TPU v7x, 256 devices: a whole 4x4x8 slice. The times are simulated.
256 devices in a mesh: tm: 64 (over x, z, core), env: 4 (over y).
Axes of the slice: x: 4, y: 4, z: 8, core: 2. Of those that a mesh axis runs over, the one named last changes fastest.
Arguments:
- init_state: float32 [70, 1024], P(None, 'env'), may hold values from -6 to 6
- torque: float32 [256, 35, 1024], P('tm', None, 'env'), may hold values from -192 to 192
- contact: int32 [256, 1024], P('tm', 'env'), may hold values 0 or 1
- mass_inverse: float32 [128, 35, 35], P('tm'), may hold values from -0.014 to 1.5, as said below
- stiffness: float32 [35], replicated, may hold values from 10 to 100
- damping: float32 [35], replicated, may hold values from 0.5 to 5
- gravity: float32 [35], replicated, may hold values from 1 to 10
- contact_stiffness: float32 [35], replicated, may hold values from 20 to 100
- contact_damping: float32 [35], replicated, may hold values from 0.5 to 3
Outputs:
- final_states: float32 [128, 70, 1024], P('tm', None, 'env')
- corrections: float32 [3, 1024], P(None, 'env')
Inputs may be any that keep to these rules, and one draw needn't show every extreme that they name: `mass_inverse`: each matrix is symmetric, and each diagonal entry exceeds the sum of the magnitudes of the other entries of its row.
All inputs are finite; a program needn't handle non-finite values. No bound on the sum of `contact` on one device may be relied on, other than what follows from the above.
Results may differ from a plain program's by a relative error of at most 0.00025.
Values sent between devices are 32-bit elements; how exact they have to be, the bound alone decides.
A program may use at most 64 MiB of HBM per device.

v0:
```python
import functools
import math

import jax
import jax.numpy as jnp
from jax import lax
from jax.experimental import pallas as pl
from jax.experimental.pallas import tpu as pltpu
from jax.sharding import PartitionSpec as P

DOF = 35
HS = 2
SUB = 32
ITERS = 3
LANES = 128
WIDE = 256

step_length = 0.05
fine_dt = step_length / SUB
TWO_PI = 2.0 * math.pi
MESH = pl.DeviceIdType.MESH
F32 = jnp.float32
BF16 = jnp.bfloat16

SIN = (
    6.283182818551188, -41.341421398631915, 81.59618387021051,
    -76.58010048603072, 41.205394649903326, -12.271261959178284,
)


def exchange_in(tm, env, tx, m2, row, rx, mall, rows, tsend, trecv, msend, mrecv, rsend, rrecv):
    me_t = lax.axis_index("tm")
    me_e = lax.axis_index("env")
    barrier = pltpu.get_barrier_semaphore()

    def peer(k):
        return {
            "tm": lax.rem(me_t + k // env, tm),
            "env": lax.rem(me_e + lax.rem(k, env), env),
        }

    @pl.loop(1, tm * env)
    def _(k):
        pl.semaphore_signal(barrier, inc=1, device_id=peer(k), device_id_type=MESH)

    pl.semaphore_wait(barrier, tm * env - 1)

    def row_copy(k):
        return pltpu.make_async_remote_copy(
            src_ref=row,
            dst_ref=rows.at[me_t, me_e],
            send_sem=rsend.at[k],
            recv_sem=rrecv.at[k],
            device_id=peer(k),
            device_id_type=MESH,
        )

    def pair(k):
        dst = lax.rem(me_t + k, tm)
        return (
            pltpu.make_async_remote_copy(
                src_ref=m2,
                dst_ref=mall.at[me_t],
                send_sem=msend.at[k],
                recv_sem=mrecv.at[k],
                device_id={"tm": dst, "env": me_e},
                device_id_type=MESH,
            ),
            pltpu.make_async_remote_copy(
                src_ref=tx.at[dst],
                dst_ref=rx.at[me_t],
                send_sem=tsend.at[k],
                recv_sem=trecv.at[k],
                device_id={"tm": dst, "env": me_e},
                device_id_type=MESH,
            ),
        )

    @pl.loop(1, tm * env)
    def _(k):
        row_copy(k).start()

    @pl.loop(1, tm)
    def _(k):
        first, second = pair(k)
        first.start()
        second.start()

    rows[me_t, me_e] = row[...]
    mall[me_t] = m2[...]
    rx[me_t] = tx[me_t]

    @pl.loop(1, tm * env)
    def _(k):
        row_copy(k).wait()

    @pl.loop(1, tm)
    def _(k):
        first, second = pair(k)
        first.wait()
        second.wait()


def exchange_out(tm, tx, rx, send, recv):
    me_t = lax.axis_index("tm")
    me_e = lax.axis_index("env")
    barrier = pltpu.get_barrier_semaphore()

    @pl.loop(1, tm)
    def _(k):
        dst = lax.rem(me_t + k, tm)
        pl.semaphore_signal(
            barrier, inc=1, device_id={"tm": dst, "env": me_e}, device_id_type=MESH
        )

    pl.semaphore_wait(barrier, tm - 1)

    def copy(k):
        dst = lax.rem(me_t + k, tm)
        return pltpu.make_async_remote_copy(
            src_ref=tx.at[dst],
            dst_ref=rx.at[me_t],
            send_sem=send.at[k],
            recv_sem=recv.at[k],
            device_id={"tm": dst, "env": me_e},
            device_id_type=MESH,
        )

    @pl.loop(1, tm)
    def _(k):
        copy(k).start()

    rx[me_t] = tx[me_t]

    @pl.loop(1, tm)
    def _(k):
        copy(k).wait()


def split(value):
    high = value.astype(BF16)
    return high, (value - high.astype(F32)).astype(BF16)


def dot(left, right):
    return jnp.dot(left, right, preferred_element_type=F32)


class Plan:
    def __init__(self, slices):
        per = LANES // DOF
        self.groups = []
        self.where = []
        base = 0
        for first in range(0, slices, per):
            count = min(per, slices - first)
            width = -(-count * DOF // LANES) * LANES
            self.groups.append((base, width, first, count))
            for pos in range(count):
                self.where.append(base + pos * DOF)
            base += width
        self.lanes = base


def compute(
    slices, local, total_env,
    rx, mall, rows, stiff, damp, gravity, cstiff, cdamp,
    out,
    tq, spring, fric, grav, cspring, cfric, wgt, wtmp, ybuf, ubuf, by, bu, ly, lu, cmap, pmap, ctmp, xs,
):
    plan = Plan(slices)
    epd = rx.shape[1]
    ratio = float(SUB)
    block = 4 if slices % 4 == 0 else 1
    unroll = max(1, min(SUB, 96 // len(plan.groups)))
    stiff, damp, gravity, cstiff, cdamp = (r[...] for r in (stiff, damp, gravity, cstiff, cdamp))
    to_u = TWO_PI / fine_dt

    for ref in (tq, spring, fric, grav, cspring, cfric, ybuf, ubuf, ly, lu):
        ref[...] = jnp.zeros(ref.shape, ref.dtype)
    ctmp[...] = jnp.zeros(ctmp.shape, F32)
    xs[...] = jnp.zeros(xs.shape, F32)

    sums = jnp.sum(rows[...], axis=1)[:, 0, :] * (1.0 / total_env)
    for n in range(slices):
        src, pos = divmod(n, local)
        at = plan.where[n]
        cut = pl.ds(at, DOF)
        grav[:, cut] = jnp.broadcast_to(gravity, (1, DOF))
        for j in range(HS):
            step = pos * HS + j
            lane = local * HS * DOF + step
            hit = rx[src, :, lane : lane + 1]
            mean = sums[src : src + 1, step : step + 1]
            tq[j, :, cut] = rx[src, :, step * DOF : (step + 1) * DOF]
            spring[j, :, cut] = TWO_PI * (stiff + hit * cstiff)
            fric[j, :, cut] = to_u * (damp + hit * cdamp)
            cspring[j, :, cut] = TWO_PI * (stiff + gravity + mean * cstiff)
            cfric[j, :, cut] = to_u * (damp + mean * cdamp)

    for g, (base, width, first, count) in enumerate(plan.groups):
        wtmp[...] = jnp.zeros(wtmp.shape, F32)
        for pos in range(count):
            src, here = divmod(first + pos, local)
            wtmp[pl.ds(pos * DOF, DOF), pl.ds(pos * DOF, DOF)] = (
                fine_dt * fine_dt / TWO_PI
            ) * mall[src, :, here * DOF : (here + 1) * DOF]
        high, low = split(wtmp[...])
        wgt[g, 0:LANES, 0:LANES] = high
        wgt[g, LANES:, 0:LANES] = high
        wgt[g, 0:LANES, LANES:] = low
        wgt[g, LANES:, LANES:] = jnp.zeros_like(low)

    def product(force, g, width):
        high, low = split(force)
        both = dot(jnp.concatenate([high, low], axis=1), wgt[g])
        return both[:, :LANES] + both[:, LANES:]

    rank = lax.broadcasted_iota(jnp.int32, (ly.shape[0], DOF), 0)
    col = lax.broadcasted_iota(jnp.int32, (ly.shape[0], DOF), 1)
    for n in range(slices):
        cut = pl.ds(plan.where[n], DOF)
        ly[:, cut] = jnp.where(rank == col, 1.0, 0.0)
        lu[:, cut] = jnp.where(rank == col + DOF, 1.0, 0.0)
    for g, (base, width, first, count) in enumerate(plan.groups):
        cut = pl.ds(base, width)
        y, u = ly[:, cut], lu[:, cut]
        for j in range(HS):
            force = -cspring[j, :, cut] * y - cfric[j, :, cut] * u
            u = u + ratio * product(force, g, width)
            y = y + ratio * u
        ly[:, cut] = y
        lu[:, cut] = u
        u = ratio * product(tq[0, :, cut], g, width)
        y = ratio * u
        for j in range(1, HS):
            force = tq[j, :, cut] - cspring[j, :, cut] * y - cfric[j, :, cut] * u
            u = u + ratio * product(force, g, width)
            y = y + ratio * u
        by[:, cut] = y
        bu[:, cut] = u
    cmap[...] = jnp.zeros(cmap.shape, BF16)
    depth = ly.shape[0]
    for n in range(slices):
        cut = pl.ds(plan.where[n], DOF)
        ctmp[0:depth, 0:DOF] = ly[:, cut]
        ctmp[0:depth, DOF : 2 * DOF] = lu[:, cut]
        high, low = split(ctmp[...])
        cmap[n, 0:LANES, 0:LANES] = high
        cmap[n, LANES:, 0:LANES] = high
        cmap[n, 0:LANES, LANES:] = low

    def through(state, weight):
        high, low = split(state)
        both = dot(jnp.concatenate([high, low], axis=1), weight)
        return both[:, :LANES] + both[:, LANES:]

    firsts = range(0, slices, block)
    running = {m: jnp.concatenate(
        [ly[:, pl.ds(plan.where[m], DOF)], lu[:, pl.ds(plan.where[m], DOF)],
         jnp.zeros((depth, LANES - 2 * DOF), F32)], axis=1) for m in firsts}
    for i in range(1, block):
        for m in firsts:
            running[m] = through(running[m], cmap[m + i])
            ctmp[0:depth, :] = running[m]
            high, low = split(ctmp[...])
            pmap[m + i, 0:LANES, 0:LANES] = high
            pmap[m + i, LANES:, 0:LANES] = high
            pmap[m + i, 0:LANES, LANES:] = low
            pmap[m + i, LANES:, LANES:] = jnp.zeros_like(low)

    def sweep(offsets, entry):
        ends = list(offsets)
        for i in range(1, block):
            for m in firsts:
                ends[m + i] = through(ends[m + i - 1], cmap[m + i]) + ends[m + i]
        enter = {}
        for m in firsts:
            enter[m] = entry
            last = m + block - 1
            whole = pmap if block > 1 else cmap
            if entry is not None:
                ends[last] = ends[last] + through(entry, whole[last])
            entry = ends[last]
        for i in range(block - 1):
            for m in firsts:
                if enter[m] is not None:
                    part = cmap if i == 0 else pmap
                    ends[m + i] = ends[m + i] + through(enter[m], part[m + i])
        return ends

    def packed(yref, uref, n):
        cut = pl.ds(plan.where[n], DOF)
        zero = jnp.zeros((epd, LANES - 2 * DOF), F32)
        return jnp.concatenate([yref[:, cut], uref[:, cut], zero], axis=1)

    lane_of = lax.broadcasted_iota(jnp.int32, (1, LANES), 1)
    scale = jnp.where(lane_of < DOF, TWO_PI, to_u)
    shrink = jnp.where(lane_of < DOF, 1.0 / TWO_PI, 1.0 / to_u)
    first_lane = local * HS * (DOF + 1)
    own = rx[lax.axis_index("tm")][:, first_lane : first_lane + 2 * DOF]
    state = jnp.concatenate([own, jnp.zeros((epd, LANES - 2 * DOF), F32)], axis=1) * shrink
    xs[0] = state
    ends = sweep([packed(by, bu, n) for n in range(slices)], state)
    for n in range(slices):
        xs[n + 1] = ends[n]

    def iteration(k, corrections):
        for n in range(slices):
            cut = pl.ds(plan.where[n], DOF)
            ybuf[:, cut] = xs[n, :, 0:DOF]
            ubuf[:, cut] = xs[n, :, DOF : 2 * DOF]
        for j in range(HS):

            def substep(counter, carry):
                result = []
                for g, (base, width, first, count) in enumerate(plan.groups):
                    y, u = carry[g]
                    cut = pl.ds(base, width)
                    t = y - jnp.round(y)
                    s = t * t
                    poly = jnp.full_like(s, SIN[-1])
                    for c in SIN[-2::-1]:
                        poly = poly * s + c
                    force = (
                        tq[j, :, cut]
                        - spring[j, :, cut] * y
                        - fric[j, :, cut] * u
                        - (grav[:, cut] * t) * poly
                    )
                    u = u + product(force, g, width)
                    y = y + u
                    result.append((y, u))
                return tuple(result)

            first_state = tuple(
                (ybuf[:, pl.ds(base, width)], ubuf[:, pl.ds(base, width)])
                for base, width, first, count in plan.groups
            )
            last = lax.fori_loop(0, SUB, substep, first_state, unroll=unroll)
            for g, (base, width, first, count) in enumerate(plan.groups):
                ybuf[:, pl.ds(base, width)] = last[g][0]
                ubuf[:, pl.ds(base, width)] = last[g][1]
        worst = jnp.zeros((epd, 1), F32)
        changes = sweep([packed(ybuf, ubuf, n) - xs[n + 1] for n in range(slices)], None)
        for n in range(slices):
            real = changes[n] * scale
            worst = jnp.maximum(worst, jnp.sum(real * real, axis=1, keepdims=True))
            xs[n + 1] = xs[n + 1] + changes[n]
        return jnp.where(lane_of == k, jnp.sqrt(worst), corrections)

    corrections = lax.fori_loop(0, ITERS, iteration, jnp.zeros((epd, LANES), F32))
    rows_of = 2 * DOF
    for n in range(slices):
        dst, pos = divmod(n, local)
        out[dst, :, pos * rows_of : (pos + 1) * rows_of] = (xs[n + 1] * scale)[:, :rows_of]
    for dst in range(slices // local):
        out[dst, :, local * rows_of : local * rows_of + ITERS] = corrections[:, :ITERS]


def body(tm, env, init_state, torque, contact, mass_inverse, stiffness, damping, gravity,
         contact_stiffness, contact_damping):
    local = mass_inverse.shape[0]
    steps = torque.shape[0]
    env_local = init_state.shape[1]
    epd = env_local // tm
    slices = local * tm
    plan = Plan(slices)
    vmem = pl.BlockSpec(memory_space=pltpu.VMEM)
    dma = pltpu.SemaphoreType.DMA

    flat = jnp.concatenate(
        [torque.reshape(steps * DOF, env_local), contact.astype(F32), init_state], axis=0
    ).T
    wide = flat.shape[1]
    tx = flat.reshape(tm, epd, wide)
    m2 = mass_inverse.transpose(1, 0, 2).reshape(DOF, local * DOF)
    row = jnp.pad(jnp.sum(contact.astype(F32), axis=1)[None], ((0, 0), (0, LANES - steps)))
    rx, mall, rows = pl.pallas_call(
        functools.partial(exchange_in, tm, env),
        out_shape=(
            jax.ShapeDtypeStruct(tx.shape, F32),
            jax.ShapeDtypeStruct((tm,) + m2.shape, F32),
            jax.ShapeDtypeStruct((tm, env, 1, LANES), F32),
        ),
        in_specs=[vmem] * 3,
        out_specs=(vmem,) * 3,
        scratch_shapes=[dma((tm,))] * 4 + [dma((tm * env,))] * 2,
        compiler_params=pltpu.CompilerParams(collective_id=0, has_side_effects=True),
        name="exchange_in",
    )(tx, m2, row)

    prm = [p.reshape(1, DOF) for p in (stiffness, damping, gravity, contact_stiffness, contact_damping)]
    depth = -(-2 * DOF // 8) * 8
    lanes = plan.lanes
    groups = len(plan.groups)
    width_out = local * 2 * DOF + ITERS
    big = pltpu.VMEM((epd, lanes), F32)
    both = pltpu.VMEM((HS, epd, lanes), F32)
    thin = pltpu.VMEM((HS, 1, lanes), F32)
    out = pl.pallas_call(
        functools.partial(compute, slices, local, env_local * env),
        out_shape=jax.ShapeDtypeStruct((tm, epd, width_out), F32),
        in_specs=[vmem] * 8,
        out_specs=vmem,
        scratch_shapes=[
            both, both, both, pltpu.VMEM((1, lanes), F32), thin, thin,
            pltpu.VMEM((groups, WIDE, WIDE), BF16),
            pltpu.VMEM((LANES, LANES), F32),
            big, big, big, big,
            pltpu.VMEM((depth, lanes), F32), pltpu.VMEM((depth, lanes), F32),
            pltpu.VMEM((slices, 2 * LANES, 2 * LANES), BF16),
            pltpu.VMEM((slices, 2 * LANES, 2 * LANES), BF16),
            pltpu.VMEM((LANES, LANES), F32),
            pltpu.VMEM((slices + 1, epd, LANES), F32),
        ],
        name="parareal",
    )(rx, mall, rows, *prm)

    back = pl.pallas_call(
        functools.partial(exchange_out, tm),
        out_shape=jax.ShapeDtypeStruct(out.shape, F32),
        in_specs=[vmem],
        out_specs=vmem,
        scratch_shapes=[dma((tm,))] * 2,
        compiler_params=pltpu.CompilerParams(collective_id=1, has_side_effects=True),
        name="exchange_out",
    )(out)
    turned = back.reshape(env_local, width_out).T
    states = turned[: local * 2 * DOF].reshape(local, 2 * DOF, env_local)
    return states, turned[local * 2 * DOF :]


def solution(mesh):
    placed = (
        P(None, "env"),
        P("tm", None, "env"),
        P("tm", "env"),
        P("tm", None, None),
        P(),
        P(),
        P(),
        P(),
        P(),
    )
    return jax.shard_map(
        functools.partial(body, mesh.shape["tm"], mesh.shape["env"]),
        mesh=mesh,
        in_specs=placed,
        out_specs=(P("tm", None, "env"), P(None, "env")),
        check_vma=False,
    )
```

profile of v0, /device:TPU:1, one launch (start us, length us, event | category | flops | bytes accessed | tf_op | source)
XLA Modules:
  0.0 286.4 jit_solution(6391504097647153970)
XLA Ops:
  0.6 0.8 convert_reduce_fusion
  1.4 0.5 pad.4.row
  2.0 0.7 convert_element_type.6
  2.6 1.5 reshape.36.m2
  4.1 0.9 copy.14
  5.1 0.9 maximum_bitcast_fusion
  6.0 0.1 copy.15
  6.1 0.8 reshape.35.tx
  6.9 63.0 %exchange_in.1 = (f32[64,4,214]{2,1,0:T(4,128)}, f32[64,35,70]{2,1,0:T(8,128)}, f32[64,4,1,128]{3,2,1,0:T(1,128)}) custom-call(f32[64,4,214]{2,1,0:T(4,128)} %reshape.35.tx, f32[35,70]{1,0:T(8,128)} %reshape.36.m2, f32[1,128]{1,0:T(1,128)} %pad.4.row), custom_call_target="tpu_custom_call" | custom-call | tf_op jit(solution)/shard_map/exchange_in/pallas_call | solution.py:379
  69.9 196.6 %parareal.1.tx = f32[64,4,143]{2,1,0:T(4,128)} custom-call(f32[64,4,214]{2,1,0:T(4,128)} %get-tuple-element.5.rx, f32[64,35,70]{2,1,0:T(8,128)} %get-tuple-element.6.mall, f32[64,4,1,128]{3,2,1,0:T(1,128)} %get-tuple-element.7.rows, f32[1,35]{1,0:T(1,128)} %bitcast.16, f32[1,35]{1,0:T(1,128)} %bitcast.17, f32[1,35]{1,0:T(1,128)} %bitcast.18, ...), custom_call_target="tpu_custom_call" | custom-call | tf_op jit(solution)/shard_map/parareal/pallas_call | solution.py:401
  266.5 17.0 %exchange_out.1 = f32[64,4,143]{2,1,0:T(4,128)} custom-call(f32[64,4,143]{2,1,0:T(4,128)} %parareal.1.tx), custom_call_target="tpu_custom_call" | custom-call | tf_op jit(solution)/shard_map/exchange_out/pallas_call | solution.py:420
  283.5 1.0 reshape.42
  284.6 0.1 slice.9
  284.7 0.7 copy.18
  285.4 0.2 reshape.44
  285.6 0.8 copy.17
  (1 shorter events, 0.0 us)
where the time goes:
time: 287 us; the launch traced here: 286 us
  Pallas kernels  277 us (97%)
  local copies, waits for them, and re-layouts  6.65 us (2%)
    pallas_call x1, Pallas kernels, body(): pl.pallas_call(functools.partial(compute, slices, local, env_local * env)...  197 us
    pallas_call x1, Pallas kernels, body(): pl.pallas_call(functools.partial(exchange_in, tm, env), out_shape=(jax.Sh...  63 us
    pallas_call x1, Pallas kernels, body(): pl.pallas_call(functools.partial(exchange_out, tm), out_shape=jax.ShapeDt...  17 us

commit v1 on v0

v1 whole, which is shorter than its diff:
```python
import functools
import math

import jax
import jax.numpy as jnp
from jax import lax
from jax.experimental import pallas as pl
from jax.experimental.pallas import tpu as pltpu
from jax.sharding import PartitionSpec as P

DOF = 35
STATE = 70
HS = 2
SUB = 32
ITERS = 3
LANES = 128
WIDE = 256
NZ = 8
CORES = 2
BLOCK = 4
UNROLL = 8

step_length = 0.05
fine_dt = step_length / SUB
TWO_PI = 2.0 * math.pi
MESH = pl.DeviceIdType.MESH
F32 = jnp.float32
BF16 = jnp.bfloat16

SIN = (
    6.283182818551188, -41.341421398631915, 81.59618387021051,
    -76.58010048603072, 41.205394649903326, -12.271261959178284,
)

ROWS_IN = 80
ROWS_OUT = 40
DEPTH = 72


def split(value):
    high = value.astype(BF16)
    return high, (value - high.astype(F32)).astype(BF16)


def dot(left, right):
    return jnp.dot(left, right, preferred_element_type=F32)


def through(state, weight):
    high, low = split(state)
    both = dot(jnp.concatenate([high, low], axis=1), weight)
    return both[:, :LANES] + both[:, LANES:]


def put(ref, n, value):
    high, low = split(value)
    ref[n, 0:LANES, 0:LANES] = high
    ref[n, LANES:, 0:LANES] = high
    ref[n, 0:LANES, LANES:] = low
    ref[n, LANES:, LANES:] = jnp.zeros_like(low)


def pad_rows(value, rows):
    return jnp.concatenate([value, jnp.zeros((rows - value.shape[0], value.shape[1]), F32)], axis=0)


class Plan:
    def __init__(self, slices):
        per = LANES // DOF
        self.groups = []
        self.where = []
        for first in range(0, slices, per):
            count = min(per, slices - first)
            base = len(self.groups) * LANES
            self.groups.append((base, first, count))
            for pos in range(count):
                self.where.append(base + pos * DOF)
        self.lanes = len(self.groups) * LANES


def kernel(
    tm, ny,
    init, torque, contact, minv, stiff, damp, gravity, cstiff, cdamp,
    out, corr_out,
    tx, rx, rowtx, rows, raw, inits,
    tq, spring, fric, grav, cspring, cfric, wgt, wtmp, ybuf, ubuf, ly, lu,
    cmap, pmap, qmap, bmap, ctmp, xs, ends_buf,
    btx, brx, stx, srx, otx, orx, ctx, crx,
    tsend, trecv, rsend, rrecv, bsend, brecv, ssend, srecv, osend, orecv, csend, crecv,
):
    nz = NZ
    half = nz // 2
    line = nz * CORES
    blocks = tm // line * CORES
    env_local = init.shape[1]
    epd = env_local // nz
    slices = HS * nz
    per_tile = LANES // epd
    tiles = env_local // LANES
    plan = Plan(slices)
    me_t = lax.axis_index("tm")
    me_e = lax.axis_index("env")
    x = me_t // line
    z = lax.rem(me_t // CORES, nz)
    c = lax.rem(me_t, CORES)
    block_t = x * CORES + c
    dest_core = z // half
    my_source = lax.rem(z, half) * CORES + c
    own_here = dest_core == c
    barrier = pltpu.get_barrier_semaphore()

    def source_index(i):
        return x * line + (c * half + i // CORES) * CORES + lax.rem(i, CORES)

    def dest_index(k):
        return x * line + lax.rem(z + k, nz) * CORES + dest_core

    def block_index(t):
        return t // CORES * line + z * CORES + lax.rem(t, CORES)

    @pl.loop(1, tm)
    def _(k):
        pl.semaphore_signal(
            barrier, inc=1, device_id={"tm": lax.rem(me_t + k, tm), "env": me_e}, device_id_type=MESH
        )

    @pl.loop(1, ny)
    def _(r):
        @pl.loop(0, nz)
        def _(i):
            pl.semaphore_signal(
                barrier, inc=1,
                device_id={"tm": source_index(i), "env": lax.rem(me_e + r, ny)},
                device_id_type=MESH,
            )

    lane_of = lax.broadcasted_iota(jnp.int32, (1, LANES), 1)
    lane_group = lane_of // epd

    raw[...] = jnp.zeros(raw.shape, F32)
    hits = contact[...].astype(F32)
    for k in range(2 * HS):
        raw[k, 0:DOF, :] = torque[:, k, :]
        raw[k, DOF : DOF + 1, :] = hits[k : k + 1, :]
    mtx = raw[0, :, 0:LANES] * 0.0
    wtmp[...] = jnp.zeros(wtmp.shape, F32)
    wtmp[0:DOF, 0:DOF] = minv[:, 0, :]
    wtmp[0:DOF, LANES // 2 : LANES // 2 + DOF] = minv[:, 1, :]
    mtx = wtmp[0:40, :]
    for h in range(tiles):
        rolled = {}
        for k in range(2 * HS):
            v = raw[k, :, h * LANES : (h + 1) * LANES]
            for r in range(per_tile):
                rolled[k, r] = v if r == 0 else pltpu.roll(v, r * epd, 1)
        for q in range(per_tile):
            acc = rolled[0, (0 - q) % per_tile]
            for k in range(1, 2 * HS):
                acc = jnp.where(lane_group == k, rolled[k, (k - q) % per_tile], acc)
            tx[h * per_tile + q, 0:40, :] = acc
            tx[h * per_tile + q, 40:80, :] = mtx
    rowtx[...] = jnp.zeros(rowtx.shape, F32)
    rowtx[0 : 2 * HS, :] = jnp.broadcast_to(jnp.sum(hits, axis=1, keepdims=True), (2 * HS, LANES))

    pl.semaphore_wait(barrier, tm - 1 + (ny - 1) * nz)

    def in_copy(k):
        return pltpu.make_async_remote_copy(
            src_ref=tx.at[lax.rem(z + k, nz)],
            dst_ref=rx.at[my_source],
            send_sem=tsend.at[k],
            recv_sem=trecv.at[my_source],
            device_id={"tm": dest_index(k), "env": me_e},
            device_id_type=MESH,
        )

    def in_arrival(i):
        return pltpu.make_async_remote_copy(
            src_ref=tx.at[0],
            dst_ref=rx.at[i],
            send_sem=tsend.at[0],
            recv_sem=trecv.at[i],
            device_id={"tm": dest_index(0), "env": me_e},
            device_id_type=MESH,
        )

    def row_copy(k, r):
        return pltpu.make_async_remote_copy(
            src_ref=rowtx,
            dst_ref=rows.at[my_source, me_e],
            send_sem=rsend.at[k, r],
            recv_sem=rrecv.at[my_source, r],
            device_id={"tm": dest_index(k), "env": lax.rem(me_e + r, ny)},
            device_id_type=MESH,
        )

    def row_arrival(i, r):
        return pltpu.make_async_remote_copy(
            src_ref=rowtx,
            dst_ref=rows.at[i, lax.rem(me_e - r + ny, ny)],
            send_sem=rsend.at[0, r],
            recv_sem=rrecv.at[i, r],
            device_id={"tm": dest_index(0), "env": lax.rem(me_e + r, ny)},
            device_id_type=MESH,
        )

    def other(k):
        return jnp.logical_not(jnp.logical_and(own_here, k == 0))

    def other_source(i):
        return jnp.logical_not(jnp.logical_and(own_here, i == my_source))

    @pl.loop(0, nz)
    def _(k):
        @pl.when(other(k))
        def _():
            in_copy(k).start()
            row_copy(k, 0).start()

        @pl.loop(1, ny)
        def _(r):
            row_copy(k, r).start()

    @pl.when(own_here)
    def _():
        rx[my_source] = tx[z]
        rows[my_source, me_e] = rowtx[...]

    ratio = float(SUB)
    stiff, damp, gravity, cstiff, cdamp = (r[...] for r in (stiff, damp, gravity, cstiff, cdamp))
    to_u = TWO_PI / fine_dt
    scale = jnp.where(lane_of < DOF, TWO_PI, to_u)
    shrink = jnp.where(lane_of < DOF, 1.0 / TWO_PI, 1.0 / to_u)

    for ref in (tq, spring, fric, grav, cspring, cfric, ybuf, ubuf, ly, lu):
        ref[...] = jnp.zeros(ref.shape, ref.dtype)
    ctmp[...] = jnp.zeros(ctmp.shape, F32)
    for h in range(tiles):
        inits[h * LANES : (h + 1) * LANES, :] = (
            pad_rows(init[:, h * LANES : (h + 1) * LANES], LANES).T * shrink
        )
    start_state = inits[pl.ds(pl.multiple_of(z * epd, epd), epd), :]
    deep = DEPTH + epd
    rank = lax.broadcasted_iota(jnp.int32, (deep, DOF), 0)
    col = lax.broadcasted_iota(jnp.int32, (deep, DOF), 1)
    for n in range(slices):
        cut = pl.ds(plan.where[n], DOF)
        ly[:, cut] = jnp.where(rank == col, 1.0, 0.0)
        lu[:, cut] = jnp.where(rank == col + DOF, 1.0, 0.0)
        grav[:, cut] = jnp.broadcast_to(gravity, (1, DOF))

    @pl.loop(0, nz)
    def _(i):
        @pl.when(other_source(i))
        def _():
            in_arrival(i).wait_recv()
            row_arrival(i, 0).wait_recv()

        @pl.loop(1, ny)
        def _(r):
            row_arrival(i, r).wait_recv()

    for i in range(nz):
        turned = pad_rows(rx[i], LANES).T
        means = jnp.sum(rows[i], axis=0)[0 : 2 * HS, 0:DOF] * (1.0 / (env_local * ny))
        for a in range(HS):
            cut = pl.ds(plan.where[HS * i + a], DOF)
            for j in range(HS):
                k = a * HS + j
                piece = turned[k * epd : (k + 1) * epd, :]
                hit = piece[:, DOF : DOF + 1]
                mean = means[k : k + 1, :]
                tq[j, :, cut] = piece[:, 0:DOF]
                spring[j, :, cut] = TWO_PI * (stiff + hit * cstiff)
                fric[j, :, cut] = to_u * (damp + hit * cdamp)
                cspring[j, :, cut] = TWO_PI * (stiff + gravity + mean * cstiff)
                cfric[j, :, cut] = to_u * (damp + mean * cdamp)

    for g, (base, first, count) in enumerate(plan.groups):
        wtmp[...] = jnp.zeros(wtmp.shape, F32)
        for pos in range(count):
            src, a = divmod(first + pos, HS)
            lane = a * (LANES // 2)
            wtmp[pl.ds(pos * DOF, DOF), pl.ds(pos * DOF, DOF)] = (
                fine_dt * fine_dt / TWO_PI
            ) * rx[src, 40 : 40 + DOF, lane : lane + DOF]
        put(wgt, g, wtmp[...])

    def product(force, g):
        return through(force, wgt[g])

    for g, (base, first, count) in enumerate(plan.groups):
        cut = pl.ds(base, LANES)
        y, u = ly[:, cut], lu[:, cut]
        for j in range(HS):
            push = jnp.concatenate([jnp.zeros((DEPTH, LANES), F32), tq[j, :, cut]], axis=0)
            force = push - cspring[j, :, cut] * y - cfric[j, :, cut] * u
            u = u + ratio * product(force, g)
            y = y + ratio * u
        ly[:, cut] = y
        lu[:, cut] = u
    offsets = []
    for n in range(slices):
        cut = pl.ds(plan.where[n], DOF)
        ctmp[0:DEPTH, 0:DOF] = ly[0:DEPTH, cut]
        ctmp[0:DEPTH, DOF : 2 * DOF] = lu[0:DEPTH, cut]
        put(cmap, n, ctmp[...])
        xs[n + 1, :, :] = jnp.zeros((epd, LANES), F32)
        xs[n + 1, :, 0:DOF] = ly[DEPTH:, cut]
        xs[n + 1, :, DOF : 2 * DOF] = lu[DEPTH:, cut]

    firsts = list(range(0, slices, BLOCK))
    running = {}
    for m in firsts:
        cut = pl.ds(plan.where[m], DOF)
        ctmp[0:DEPTH, 0:DOF] = ly[0:DEPTH, cut]
        ctmp[0:DEPTH, DOF : 2 * DOF] = lu[0:DEPTH, cut]
        running[m] = ctmp[0:DEPTH, :]
    whole = running[0]
    put(qmap, 0, pad_rows(running[0], LANES))
    for i in range(1, BLOCK):
        for m in firsts:
            running[m] = through(running[m], cmap[m + i])
            put(pmap, m + i, pad_rows(running[m], LANES))
            if m == 0:
                put(qmap, i, pad_rows(running[m], LANES))
    whole = running[0]
    for m in firsts[1:]:
        entry = whole
        for i in range(BLOCK):
            part = cmap if i == 0 else pmap
            whole = through(entry, part[m + i])
            put(qmap, m + i, pad_rows(whole, LANES))

    def sweep_to_end(ends):
        for i in range(1, BLOCK):
            for m in firsts:
                ends[m + i] = through(ends[m + i - 1], cmap[m + i]) + ends[m + i]
        for m in firsts[1:]:
            last = m + BLOCK - 1
            ends[last] = ends[last] + through(ends[m - 1], pmap[last])

    def sweep_rest(ends):
        for i in range(BLOCK - 1):
            for m in firsts[1:]:
                part = cmap if i == 0 else pmap
                ends[m + i] = ends[m + i] + through(ends[m - 1], part[m + i])

    def first_copy(d):
        return pltpu.make_async_remote_copy(
            src_ref=btx,
            dst_ref=brx.at[block_t],
            send_sem=bsend.at[d],
            recv_sem=brecv.at[d],
            device_id={"tm": block_index(block_t + d), "env": me_e},
            device_id_type=MESH,
        )

    def first_arrival(d):
        return pltpu.make_async_remote_copy(
            src_ref=btx,
            dst_ref=brx.at[block_t - d],
            send_sem=bsend.at[d],
            recv_sem=brecv.at[d],
            device_id={"tm": block_index(block_t - d), "env": me_e},
            device_id_type=MESH,
        )

    def sweep_copy(k, d):
        return pltpu.make_async_remote_copy(
            src_ref=stx.at[k],
            dst_ref=srx.at[k, block_t],
            send_sem=ssend.at[k, d],
            recv_sem=srecv.at[k, d],
            device_id={"tm": block_index(block_t + d), "env": me_e},
            device_id_type=MESH,
        )

    def sweep_arrival(k, d):
        return pltpu.make_async_remote_copy(
            src_ref=stx.at[k],
            dst_ref=srx.at[k, block_t - d],
            send_sem=ssend.at[k, d],
            recv_sem=srecv.at[k, d],
            device_id={"tm": block_index(block_t - d), "env": me_e},
            device_id_type=MESH,
        )

    def send_blocks(copy):
        @pl.loop(1, blocks)
        def _(d):
            @pl.when(block_t + d < blocks)
            def _():
                copy(d).start()

    def await_blocks(arrival):
        @pl.loop(1, blocks)
        def _(d):
            @pl.when(block_t - d >= 0)
            def _():
                arrival(d).wait_recv()

    def drain_blocks(copy):
        @pl.loop(1, blocks)
        def _(d):
            @pl.when(block_t + d < blocks)
            def _():
                copy(d).wait_send()

    ends = [xs[n + 1] for n in range(slices)]
    sweep_to_end(ends)
    btx[0:DEPTH, :] = whole
    btx[DEPTH:, :] = ends[slices - 1]
    send_blocks(first_copy)
    sweep_rest(ends)
    for n in range(slices):
        ends_buf[n] = ends[n]
    await_blocks(first_arrival)
    for t in range(blocks - 1):
        put(bmap, t, pad_rows(brx[t, 0:DEPTH, :], LANES))

    state = start_state
    entry = start_state
    for t in range(blocks - 1):
        state = through(state, bmap[t]) + brx[t, DEPTH:, :]
        entry = jnp.where(block_t == t + 1, state, entry)
    xs[0] = entry
    for n in range(slices):
        xs[n + 1] = ends_buf[n] + through(entry, qmap[n])

    def iteration(k, corrections):
        for n in range(slices):
            cut = pl.ds(plan.where[n], DOF)
            ybuf[:, cut] = xs[n, :, 0:DOF]
            ubuf[:, cut] = xs[n, :, DOF : 2 * DOF]
        for j in range(HS):

            def substep(counter, carry):
                result = []
                for g, (base, first, count) in enumerate(plan.groups):
                    y, u = carry[g]
                    cut = pl.ds(base, LANES)
                    t = y - jnp.round(y)
                    s = t * t
                    poly = jnp.full_like(s, SIN[-1])
                    for coef in SIN[-2::-1]:
                        poly = poly * s + coef
                    force = (
                        tq[j, :, cut]
                        - spring[j, :, cut] * y
                        - fric[j, :, cut] * u
                        - (grav[:, cut] * t) * poly
                    )
                    u = u + product(force, g)
                    y = y + u
                    result.append((y, u))
                return tuple(result)

            first_state = tuple(
                (ybuf[:, pl.ds(base, LANES)], ubuf[:, pl.ds(base, LANES)])
                for base, first, count in plan.groups
            )
            last = lax.fori_loop(0, SUB, substep, first_state, unroll=UNROLL)
            for g, (base, first, count) in enumerate(plan.groups):
                ybuf[:, pl.ds(base, LANES)] = last[g][0]
                ubuf[:, pl.ds(base, LANES)] = last[g][1]

        zero = jnp.zeros((epd, LANES - 2 * DOF), F32)
        ends = []
        for n in range(slices):
            cut = pl.ds(plan.where[n], DOF)
            ends.append(jnp.concatenate([ybuf[:, cut], ubuf[:, cut], zero], axis=1) - xs[n + 1])
        sweep_to_end(ends)
        stx[k] = ends[slices - 1]
        send_blocks(functools.partial(sweep_copy, k))
        sweep_rest(ends)
        for n in range(slices):
            ends_buf[n] = ends[n]
        await_blocks(functools.partial(sweep_arrival, k))
        state = jnp.zeros((epd, LANES), F32)
        entry = state
        for t in range(blocks - 1):
            state = through(state, bmap[t]) + srx[k, t] if t > 0 else srx[k, t]
            entry = jnp.where(block_t == t + 1, state, entry)
        xs[0] = xs[0] + entry
        worst = jnp.zeros((epd, 1), F32)
        for n in range(slices):
            change = ends_buf[n] + through(entry, qmap[n])
            real = change * scale
            worst = jnp.maximum(worst, jnp.sum(real * real, axis=1, keepdims=True))
            xs[n + 1] = xs[n + 1] + change
        return jnp.where(lane_of == k, jnp.sqrt(worst), corrections)

    corrections = lax.fori_loop(0, ITERS, iteration, jnp.zeros((epd, LANES), F32))

    ctx[...] = pad_rows(corrections, LANES).T[0:8, :]
    for i in range(nz):
        parts = []
        for a in range(HS):
            real = xs[HS * i + a + 1] * scale
            parts.append(real)
            parts.append(pltpu.roll(real, LANES - DOF, 1))
        otx[i] = jnp.concatenate(parts, axis=0).T[0:ROWS_OUT, :]

    def out_copy(i):
        return pltpu.make_async_remote_copy(
            src_ref=otx.at[i],
            dst_ref=orx.at[z],
            send_sem=osend.at[i],
            recv_sem=orecv.at[z],
            device_id={"tm": source_index(i), "env": me_e},
            device_id_type=MESH,
        )

    def out_arrival(k):
        return pltpu.make_async_remote_copy(
            src_ref=otx.at[0],
            dst_ref=orx.at[lax.rem(z + k, nz)],
            send_sem=osend.at[0],
            recv_sem=orecv.at[lax.rem(z + k, nz)],
            device_id={"tm": dest_index(k), "env": me_e},
            device_id_type=MESH,
        )

    def corr_copy(k):
        return pltpu.make_async_remote_copy(
            src_ref=ctx,
            dst_ref=crx.at[block_t, z],
            send_sem=csend.at[k],
            recv_sem=crecv.at[k],
            device_id={"tm": lax.rem(me_t + k, tm), "env": me_e},
            device_id_type=MESH,
        )

    @pl.loop(1, tm)
    def _(k):
        corr_copy(k).start()

    @pl.loop(0, nz)
    def _(i):
        @pl.when(other_source(i))
        def _():
            out_copy(i).start()

    crx[block_t, z] = ctx[...]

    @pl.when(own_here)
    def _():
        orx[z] = otx[my_source]

    @pl.loop(0, nz)
    def _(k):
        @pl.when(other(k))
        def _():
            out_arrival(k).wait_recv()

    for h in range(tiles):
        for k in range(2 * HS):
            a, half_state = divmod(k, 2)
            tile = None
            for q in range(per_tile):
                r = (q - k) % per_tile
                v = orx[h * per_tile + q]
                v = v if r == 0 else pltpu.roll(v, r * epd, 1)
                tile = v if tile is None else jnp.where(lane_group == q, v, tile)
            out[half_state * DOF : half_state * DOF + DOF, a, h * LANES : (h + 1) * LANES] = tile[0:DOF]

    @pl.loop(1, tm)
    def _(k):
        corr_copy(k).wait()

    worst = crx[0]
    for t in range(1, blocks):
        worst = jnp.maximum(worst, crx[t])
    for h in range(tiles):
        tile = worst[h * per_tile]
        for q in range(1, per_tile):
            tile = jnp.where(lane_group == q, pltpu.roll(worst[h * per_tile + q], q * epd, 1), tile)
        corr_out[:, h * LANES : (h + 1) * LANES] = tile[0:ITERS]

    @pl.loop(0, nz)
    def _(k):
        @pl.when(other(k))
        def _():
            in_copy(k).wait_send()
            row_copy(k, 0).wait_send()

        @pl.loop(1, ny)
        def _(r):
            row_copy(k, r).wait_send()

        @pl.when(other_source(k))
        def _():
            out_copy(k).wait_send()

    drain_blocks(first_copy)
    for k in range(ITERS):
        drain_blocks(functools.partial(sweep_copy, k))


def body(tm, env, init_state, torque, contact, mass_inverse, stiffness, damping, gravity,
         contact_stiffness, contact_damping):
    nz = NZ
    env_local = init_state.shape[1]
    epd = env_local // nz
    slices = HS * nz
    blocks = tm // (nz * CORES) * CORES
    plan = Plan(slices)
    groups = len(plan.groups)
    lanes = plan.lanes
    vm = pltpu.VMEM
    dma = pltpu.SemaphoreType.DMA
    vmem = pl.BlockSpec(memory_space=pltpu.VMEM)
    both = vm((HS, epd, lanes), F32)
    thin = vm((HS, 1, lanes), F32)
    deep = DEPTH + epd
    prm = [p.reshape(1, DOF) for p in (stiffness, damping, gravity, contact_stiffness, contact_damping)]
    states, corrections = pl.pallas_call(
        functools.partial(kernel, tm, env),
        out_shape=(
            jax.ShapeDtypeStruct((STATE, HS, env_local), F32),
            jax.ShapeDtypeStruct((ITERS, env_local), F32),
        ),
        in_specs=[vmem] * 9,
        out_specs=(vmem, vmem),
        scratch_shapes=[
            vm((nz, ROWS_IN, LANES), F32), vm((nz, ROWS_IN, LANES), F32),
            vm((8, LANES), F32), vm((nz, env, 8, LANES), F32),
            vm((2 * HS, 40, env_local), F32), vm((env_local, LANES), F32),
            both, both, both, vm((1, lanes), F32), thin, thin,
            vm((groups, WIDE, WIDE), BF16), vm((LANES, LANES), F32),
            vm((epd, lanes), F32), vm((epd, lanes), F32),
            vm((deep, lanes), F32), vm((deep, lanes), F32),
            vm((slices, WIDE, WIDE), BF16), vm((slices, WIDE, WIDE), BF16),
            vm((slices, WIDE, WIDE), BF16), vm((blocks, WIDE, WIDE), BF16),
            vm((LANES, LANES), F32),
            vm((slices + 1, epd, LANES), F32), vm((slices, epd, LANES), F32),
            vm((deep, LANES), F32), vm((blocks, deep, LANES), F32),
            vm((ITERS, epd, LANES), F32), vm((ITERS, blocks, epd, LANES), F32),
            vm((nz, ROWS_OUT, LANES), F32), vm((nz, ROWS_OUT, LANES), F32),
            vm((8, LANES), F32), vm((blocks, nz, 8, LANES), F32),
            dma((nz,)), dma((nz,)), dma((nz, env)), dma((nz, env)),
            dma((blocks,)), dma((blocks,)), dma((ITERS, blocks)), dma((ITERS, blocks)),
            dma((nz,)), dma((nz,)), dma((tm,)), dma((tm,)),
        ],
        compiler_params=pltpu.CompilerParams(collective_id=0, has_side_effects=True),
        name="parareal",
    )(
        init_state, torque.transpose(1, 0, 2), contact, mass_inverse.transpose(1, 0, 2), *prm
    )
    return states.transpose(1, 0, 2), corrections


def solution(mesh):
    placed = (
        P(None, "env"),
        P("tm", None, "env"),
        P("tm", "env"),
        P("tm", None, None),
        P(),
        P(),
        P(),
        P(),
        P(),
    )
    return jax.shard_map(
        functools.partial(body, mesh.shape["tm"], mesh.shape["env"]),
        mesh=mesh,
        in_specs=placed,
        out_specs=(P("tm", None, "env"), P(None, "env")),
        check_vma=False,
    )
```

time: 287 us -> 96 us (0.33)
  the two profiles are of different devices: /device:TPU:1 before, /device:TPU:39 now
where the time goes in v1:
time: 96 us; the launch traced here: 95.9 us
  Pallas kernels  93.1 us (97%)
  local copies, waits for them, and re-layouts  2.17 us (2%)
    pallas_call x1, Pallas kernels, body(): pl.pallas_call(functools.partial(kernel, tm, env), out_shape=(jax.ShapeDt...  93.1 us
    unnamed x4, local copies, waits for them, and re-layouts  2.17 us

profile of v1, /device:TPU:39, one launch (start us, length us, event | category | flops | bytes accessed | tf_op | source)
XLA Modules:
  0.0 95.9 jit_solution(17386351595886402782)
XLA Ops:
  0.6 93.1 %parareal.1 = (f32[70,2,256]{2,1,0:T(2,128)}, f32[3,256]{1,0:T(4,128)}) custom-call(f32[70,256]{1,0:T(8,128)} %init.1, f32[35,4,256]{2,1,0:T(4,128)} %bitcast.9, s32[4,256]{1,0:T(4,128)} %contact.1, f32[35,2,35]{2,1,0:T(2,128)} %bitcast.10, f32[1,35]{1,0:T(1,128)} %bitcast.11, f32[1,35]{1,0:T(1,128)} %bitcast.12, f32[1,35]{1,0:T(1,128)} %bitcast.13, ...), custom_call_target="tpu_custom_call" | custom-call | tf_op jit(solution)/shard_map/parareal/pallas_call | solution.py:618
  93.7 0.0 copy-start
  93.7 1.6 %copy.13 = f32[2,70,256]{2,0,1:T(2,128)} copy(f32[2,70,256]{2,0,1:T(2,128)} %bitcast.8) | data formatting | bytes 286720
  95.3 0.0 copy-done
  95.3 0.6 copy.14
Async XLA Ops:
  93.7 1.6 %copy-start = (f32[3,256]{1,0:T(4,128)S(1)}, f32[3,256]{1,0:T(4,128)}, u32[]{:S(2)}) copy-start(f32[3,256]{1,0:T(4,128)} %get-tuple-element.9) | copy-start | bytes 9220

commit v2 on v1

--- a/solution.py
+++ b/solution.py
@@ -17,8 +17,7 @@
 WIDE = 256
 NZ = 8
 CORES = 2
-BLOCK = 4
-UNROLL = 8
+UNROLL = 32
 
 step_length = 0.05
 fine_dt = step_length / SUB
@@ -32,7 +31,9 @@
     -76.58010048603072, 41.205394649903326, -12.271261959178284,
 )
 
-ROWS_IN = 80
+ROWS_IN = 56
+FOLD = 36
+KEEP = 80
 ROWS_OUT = 40
 DEPTH = 72
 
@@ -52,12 +53,16 @@
     return both[:, :LANES] + both[:, LANES:]
 
 
+def clear(ref):
+    ref[...] = jnp.zeros(ref.shape, ref.dtype)
+
+
 def put(ref, n, value):
     high, low = split(value)
-    ref[n, 0:LANES, 0:LANES] = high
-    ref[n, LANES:, 0:LANES] = high
-    ref[n, 0:LANES, LANES:] = low
-    ref[n, LANES:, LANES:] = jnp.zeros_like(low)
+    rows = value.shape[0]
+    ref[n, 0:rows, 0:LANES] = high
+    ref[n, LANES : LANES + rows, 0:LANES] = high
+    ref[n, 0:rows, LANES:] = low
 
 
 def pad_rows(value, rows):
@@ -80,14 +85,22 @@
 
 def kernel(
     tm, ny,
+    init_hbm, torque_hbm, contact_hbm, minv_hbm, stiff_hbm, damp_hbm, gravity_hbm, cstiff_hbm, cdamp_hbm,
+    out, corr_out,
     init, torque, contact, minv, stiff, damp, gravity, cstiff, cdamp,
-    out, corr_out,
     tx, rx, rowtx, rows, raw, inits,
-    tq, spring, fric, grav, cspring, cfric, wgt, wtmp, ybuf, ubuf, ly, lu,
-    cmap, pmap, qmap, bmap, ctmp, xs, ends_buf,
+    tq, spring, fric, grav, cspring, cfric, wgt, stage, wtmp, ybuf, ubuf, ly, lu,
+    cmap, qmap, bmap, ctmp, xs, ends_buf,
     btx, brx, stx, srx, otx, orx, ctx, crx,
-    tsend, trecv, rsend, rrecv, bsend, brecv, ssend, srecv, osend, orecv, csend, crecv,
+    lsem, tsend, trecv, rsend, rrecv, bsend, brecv, ssend, srecv, osend, orecv, csend, crecv,
 ):
+    pairs = (
+        (torque_hbm, torque), (contact_hbm, contact), (minv_hbm, minv), (init_hbm, init), (stiff_hbm, stiff),
+        (damp_hbm, damp), (gravity_hbm, gravity), (cstiff_hbm, cstiff), (cdamp_hbm, cdamp),
+    )
+    local = [pltpu.make_async_copy(src, dst, lsem.at[i]) for i, (src, dst) in enumerate(pairs)]
+    for copy in local:
+        copy.start()
     nz = NZ
     half = nz // 2
     line = nz * CORES
@@ -134,6 +147,8 @@
                 device_id_type=MESH,
             )
 
+    for copy in local:
+        copy.wait()
     lane_of = lax.broadcasted_iota(jnp.int32, (1, LANES), 1)
     lane_group = lane_of // epd
 
@@ -142,11 +157,14 @@
     for k in range(2 * HS):
         raw[k, 0:DOF, :] = torque[:, k, :]
         raw[k, DOF : DOF + 1, :] = hits[k : k + 1, :]
-    mtx = raw[0, :, 0:LANES] * 0.0
     wtmp[...] = jnp.zeros(wtmp.shape, F32)
     wtmp[0:DOF, 0:DOF] = minv[:, 0, :]
-    wtmp[0:DOF, LANES // 2 : LANES // 2 + DOF] = minv[:, 1, :]
-    mtx = wtmp[0:40, :]
+    wtmp[40 : 40 + DOF, 0:DOF] = minv[:, 1, :]
+    row_of = lax.broadcasted_iota(jnp.int32, (40, LANES), 0)
+    lower = lane_of <= row_of
+    packed = jnp.where(lower, wtmp[0:40, :], pltpu.roll(wtmp[40:80, :], 1, 1))
+    last = jnp.concatenate([packed[32:40], jnp.zeros((8, LANES), F32)], axis=0)
+    mtx = packed[0:16] + pltpu.roll(packed[16:32], FOLD, 1) + pltpu.roll(last, 2 * FOLD, 1)
     for h in range(tiles):
         rolled = {}
         for k in range(2 * HS):
@@ -158,9 +176,12 @@
             for k in range(1, 2 * HS):
                 acc = jnp.where(lane_group == k, rolled[k, (k - q) % per_tile], acc)
             tx[h * per_tile + q, 0:40, :] = acc
-            tx[h * per_tile + q, 40:80, :] = mtx
-    rowtx[...] = jnp.zeros(rowtx.shape, F32)
-    rowtx[0 : 2 * HS, :] = jnp.broadcast_to(jnp.sum(hits, axis=1, keepdims=True), (2 * HS, LANES))
+            tx[h * per_tile + q, 40:ROWS_IN, :] = mtx
+    totals = jnp.sum(hits, axis=1, keepdims=True)
+    row = jnp.broadcast_to(totals[0:1], (1, LANES))
+    for k in range(1, 2 * HS):
+        row = jnp.where(lane_group == k, jnp.broadcast_to(totals[k : k + 1], (1, LANES)), row)
+    rowtx[...] = row
 
     pl.semaphore_wait(barrier, tm - 1 + (ny - 1) * nz)
 
@@ -214,12 +235,16 @@
     def _(k):
         @pl.when(other(k))
         def _():
-            in_copy(k).start()
             row_copy(k, 0).start()
 
         @pl.loop(1, ny)
         def _(r):
             row_copy(k, r).start()
+
+    for k in sorted(range(nz), key=lambda k: -min(k, nz - k)):
+        @pl.when(other(k))
+        def _(k=k):
+            in_copy(k).start()
 
     @pl.when(own_here)
     def _():
@@ -232,15 +257,15 @@
     scale = jnp.where(lane_of < DOF, TWO_PI, to_u)
     shrink = jnp.where(lane_of < DOF, 1.0 / TWO_PI, 1.0 / to_u)
 
-    for ref in (tq, spring, fric, grav, cspring, cfric, ybuf, ubuf, ly, lu):
-        ref[...] = jnp.zeros(ref.shape, ref.dtype)
-    ctmp[...] = jnp.zeros(ctmp.shape, F32)
+    for ref in (tq, spring, fric, grav, cspring, cfric, ybuf, ubuf, ly, lu, ctmp, stage, wgt, cmap, qmap, bmap):
+        clear(ref)
     for h in range(tiles):
         inits[h * LANES : (h + 1) * LANES, :] = (
             pad_rows(init[:, h * LANES : (h + 1) * LANES], LANES).T * shrink
         )
     start_state = inits[pl.ds(pl.multiple_of(z * epd, epd), epd), :]
     deep = DEPTH + epd
+    first_start = jnp.where(block_t == 0, start_state, 0.0)
     rank = lax.broadcasted_iota(jnp.int32, (deep, DOF), 0)
     col = lax.broadcasted_iota(jnp.int32, (deep, DOF), 1)
     for n in range(slices):
@@ -248,28 +273,43 @@
         ly[:, cut] = jnp.where(rank == col, 1.0, 0.0)
         lu[:, cut] = jnp.where(rank == col + DOF, 1.0, 0.0)
         grav[:, cut] = jnp.broadcast_to(gravity, (1, DOF))
-
-    @pl.loop(0, nz)
-    def _(i):
+    ly[DEPTH:, 0:DOF] = first_start[:, 0:DOF]
+    lu[DEPTH:, 0:DOF] = first_start[:, DOF : 2 * DOF]
+
+    square_row = lax.broadcasted_iota(jnp.int32, (40, LANES), 0)
+    for i in range(nz):
         @pl.when(other_source(i))
-        def _():
+        def _(i=i):
             in_arrival(i).wait_recv()
             row_arrival(i, 0).wait_recv()
 
         @pl.loop(1, ny)
-        def _(r):
+        def _(r, i=i):
             row_arrival(i, r).wait_recv()
 
-    for i in range(nz):
-        turned = pad_rows(rx[i], LANES).T
-        means = jnp.sum(rows[i], axis=0)[0 : 2 * HS, 0:DOF] * (1.0 / (env_local * ny))
+        folded = rx[i, 40:ROWS_IN, :]
+        square = jnp.concatenate(
+            [folded, pltpu.roll(folded, LANES - FOLD, 1), pltpu.roll(folded[0:8], LANES - 2 * FOLD, 1)], axis=0
+        )
+        shifted = pltpu.roll(square, LANES - 1, 1)
+        turned = jnp.concatenate([rx[i, 0:40, :], square, shifted, jnp.zeros((8, LANES), F32)], axis=0).T
+        matrices = (
+            jnp.where(lane_of <= square_row, square, pltpu.roll(turned[0:40], LANES - 40, 1)),
+            jnp.where(lane_of >= square_row, shifted, pltpu.roll(turned[0:40], LANES - 80, 1)),
+        )
+        means = jnp.sum(rows[i], axis=0) * (1.0 / (env_local * ny))
         for a in range(HS):
-            cut = pl.ds(plan.where[HS * i + a], DOF)
+            n = HS * i + a
+            cut = pl.ds(plan.where[n], DOF)
+            g, pos = divmod(n, LANES // DOF)
+            stage[g, pl.ds(pos * DOF, DOF), pl.ds(pos * DOF, DOF)] = (
+                fine_dt * fine_dt / TWO_PI
+            ) * matrices[a][0:DOF, 0:DOF]
             for j in range(HS):
                 k = a * HS + j
                 piece = turned[k * epd : (k + 1) * epd, :]
                 hit = piece[:, DOF : DOF + 1]
-                mean = means[k : k + 1, :]
+                mean = means[:, k * epd : k * epd + 1]
                 tq[j, :, cut] = piece[:, 0:DOF]
                 spring[j, :, cut] = TWO_PI * (stiff + hit * cstiff)
                 fric[j, :, cut] = to_u * (damp + hit * cdamp)
@@ -277,14 +317,7 @@
                 cfric[j, :, cut] = to_u * (damp + mean * cdamp)
 
     for g, (base, first, count) in enumerate(plan.groups):
-        wtmp[...] = jnp.zeros(wtmp.shape, F32)
-        for pos in range(count):
-            src, a = divmod(first + pos, HS)
-            lane = a * (LANES // 2)
-            wtmp[pl.ds(pos * DOF, DOF), pl.ds(pos * DOF, DOF)] = (
-                fine_dt * fine_dt / TWO_PI
-            ) * rx[src, 40 : 40 + DOF, lane : lane + DOF]
-        put(wgt, g, wtmp[...])
+        put(wgt, g, stage[g])
 
     def product(force, g):
         return through(force, wgt[g])
@@ -299,52 +332,37 @@
             y = y + ratio * u
         ly[:, cut] = y
         lu[:, cut] = u
-    offsets = []
+    levels = slices.bit_length() - 1
+    stacks = []
     for n in range(slices):
         cut = pl.ds(plan.where[n], DOF)
-        ctmp[0:DEPTH, 0:DOF] = ly[0:DEPTH, cut]
-        ctmp[0:DEPTH, DOF : 2 * DOF] = lu[0:DEPTH, cut]
-        put(cmap, n, ctmp[...])
-        xs[n + 1, :, :] = jnp.zeros((epd, LANES), F32)
-        xs[n + 1, :, 0:DOF] = ly[DEPTH:, cut]
-        xs[n + 1, :, DOF : 2 * DOF] = lu[DEPTH:, cut]
-
-    firsts = list(range(0, slices, BLOCK))
-    running = {}
-    for m in firsts:
-        cut = pl.ds(plan.where[m], DOF)
-        ctmp[0:DEPTH, 0:DOF] = ly[0:DEPTH, cut]
-        ctmp[0:DEPTH, DOF : 2 * DOF] = lu[0:DEPTH, cut]
-        running[m] = ctmp[0:DEPTH, :]
-    whole = running[0]
-    put(qmap, 0, pad_rows(running[0], LANES))
-    for i in range(1, BLOCK):
-        for m in firsts:
-            running[m] = through(running[m], cmap[m + i])
-            put(pmap, m + i, pad_rows(running[m], LANES))
-            if m == 0:
-                put(qmap, i, pad_rows(running[m], LANES))
-    whole = running[0]
-    for m in firsts[1:]:
-        entry = whole
-        for i in range(BLOCK):
-            part = cmap if i == 0 else pmap
-            whole = through(entry, part[m + i])
-            put(qmap, m + i, pad_rows(whole, LANES))
-
-    def sweep_to_end(ends):
-        for i in range(1, BLOCK):
-            for m in firsts:
-                ends[m + i] = through(ends[m + i - 1], cmap[m + i]) + ends[m + i]
-        for m in firsts[1:]:
-            last = m + BLOCK - 1
-            ends[last] = ends[last] + through(ends[m - 1], pmap[last])
-
-    def sweep_rest(ends):
-        for i in range(BLOCK - 1):
-            for m in firsts[1:]:
-                part = cmap if i == 0 else pmap
-                ends[m + i] = ends[m + i] + through(ends[m - 1], part[m + i])
+        ctmp[:, 0:DOF] = ly[:, cut]
+        ctmp[:, DOF : 2 * DOF] = lu[:, cut]
+        stacks.append(ctmp[...])
+
+    def right_half(level):
+        step = 1 << level
+        place = 0
+        for m in range(0, slices, 2 * step):
+            for i in range(step):
+                yield place, m + step - 1, m + step + i
+                place += 1
+
+    keep_offsets = lax.broadcasted_iota(jnp.int32, (deep, LANES), 0) >= DEPTH
+    for level in range(levels):
+        for place, left, n in right_half(level):
+            put(cmap, level * (slices // 2) + place, stacks[n][0:DEPTH])
+        for place, left, n in right_half(level):
+            moved = through(stacks[left], cmap[level * (slices // 2) + place])
+            stacks[n] = moved + jnp.where(keep_offsets, stacks[n], 0.0)
+    for n in range(slices):
+        put(qmap, n, stacks[n][0:DEPTH])
+    ends = [stack[DEPTH:] for stack in stacks]
+
+    def sweep(ends):
+        for level in range(levels):
+            for place, left, n in right_half(level):
+                ends[n] = ends[n] + through(ends[left], cmap[level * (slices // 2) + place])
 
     def first_copy(d):
         return pltpu.make_async_remote_copy(
@@ -407,24 +425,51 @@
             def _():
                 copy(d).wait_send()
 
-    ends = [xs[n + 1] for n in range(slices)]
-    sweep_to_end(ends)
-    btx[0:DEPTH, :] = whole
-    btx[DEPTH:, :] = ends[slices - 1]
-    send_blocks(first_copy)
-    sweep_rest(ends)
+    btx[...] = stacks[slices - 1][0:DEPTH]
+    stx[0] = ends[slices - 1]
     for n in range(slices):
         ends_buf[n] = ends[n]
+    send_blocks(first_copy)
+    send_blocks(functools.partial(sweep_copy, 0))
     await_blocks(first_arrival)
-    for t in range(blocks - 1):
-        put(bmap, t, pad_rows(brx[t, 0:DEPTH, :], LANES))
-
-    state = start_state
-    entry = start_state
-    for t in range(blocks - 1):
-        state = through(state, bmap[t]) + brx[t, DEPTH:, :]
-        entry = jnp.where(block_t == t + 1, state, entry)
-    xs[0] = entry
+    eye = jnp.where(
+        lax.broadcasted_iota(jnp.int32, (DEPTH, LANES), 0) == lane_of, 1.0, 0.0
+    )
+    maps = {t: jnp.where(t < block_t, brx[t], eye) for t in range(1, blocks - 1)}
+    pieces = {(t, t): maps[t] for t in maps}
+
+    def join(a, b, c):
+        if (a, c) not in pieces:
+            slot = weights.setdefault((b, c), len(weights))
+            if slot == len(weights) - 1:
+                put(bmap, slot, pieces[b, c])
+            pieces[a, c] = through(pieces[a, b - 1], bmap[slot])
+
+    weights = {}
+    top = blocks - 2
+    span = 1
+    while span < blocks:
+        for last in range(top, 0, -2 * span):
+            mid = last - span + 1
+            if mid <= 1:
+                continue
+            for first in range(max(1, mid - span), mid):
+                join(first, mid, last)
+        span *= 2
+    for t in range(blocks - 2):
+        if (t + 1, top) not in weights:
+            weights[t + 1, top] = len(weights)
+            put(bmap, weights[t + 1, top], pieces[t + 1, top])
+
+    def enter(k):
+        total = jnp.where(blocks - 2 < block_t, srx[k, blocks - 2], 0.0)
+        for t in range(blocks - 2):
+            total = total + through(jnp.where(t < block_t, srx[k, t], 0.0), bmap[weights[t + 1, top]])
+        return total
+
+    await_blocks(functools.partial(sweep_arrival, 0))
+    entry = enter(0)
+    xs[0] = jnp.where(block_t == 0, start_state, entry)
     for n in range(slices):
         xs[n + 1] = ends_buf[n] + through(entry, qmap[n])
 
@@ -442,9 +487,8 @@
                     cut = pl.ds(base, LANES)
                     t = y - jnp.round(y)
                     s = t * t
-                    poly = jnp.full_like(s, SIN[-1])
-                    for coef in SIN[-2::-1]:
-                        poly = poly * s + coef
+                    s2 = s * s
+                    poly = (SIN[0] + SIN[1] * s) + s2 * ((SIN[2] + SIN[3] * s) + s2 * (SIN[4] + SIN[5] * s))
                     force = (
                         tq[j, :, cut]
                         - spring[j, :, cut] * y
@@ -470,18 +514,13 @@
         for n in range(slices):
             cut = pl.ds(plan.where[n], DOF)
             ends.append(jnp.concatenate([ybuf[:, cut], ubuf[:, cut], zero], axis=1) - xs[n + 1])
-        sweep_to_end(ends)
-        stx[k] = ends[slices - 1]
-        send_blocks(functools.partial(sweep_copy, k))
-        sweep_rest(ends)
+        sweep(ends)
+        stx[k + 1] = ends[slices - 1]
         for n in range(slices):
             ends_buf[n] = ends[n]
-        await_blocks(functools.partial(sweep_arrival, k))
-        state = jnp.zeros((epd, LANES), F32)
-        entry = state
-        for t in range(blocks - 1):
-            state = through(state, bmap[t]) + srx[k, t] if t > 0 else srx[k, t]
-            entry = jnp.where(block_t == t + 1, state, entry)
+        send_blocks(functools.partial(sweep_copy, k + 1))
+        await_blocks(functools.partial(sweep_arrival, k + 1))
+        entry = enter(k + 1)
         xs[0] = xs[0] + entry
         worst = jnp.zeros((epd, 1), F32)
         for n in range(slices):
@@ -493,7 +532,11 @@
 
     corrections = lax.fori_loop(0, ITERS, iteration, jnp.zeros((epd, LANES), F32))
 
-    ctx[...] = pad_rows(corrections, LANES).T[0:8, :]
+    turned = pad_rows(corrections, LANES).T
+    row = turned[0:1]
+    for k in range(1, ITERS):
+        row = jnp.where(lane_group == k, pltpu.roll(turned[k : k + 1], k * epd, 1), row)
+    ctx[...] = row
     for i in range(nz):
         parts = []
         for a in range(HS):
@@ -532,15 +575,15 @@
             device_id_type=MESH,
         )
 
-    @pl.loop(1, tm)
-    def _(k):
-        corr_copy(k).start()
-
     @pl.loop(0, nz)
     def _(i):
         @pl.when(other_source(i))
         def _():
             out_copy(i).start()
+
+    @pl.loop(1, tm)
+    def _(k):
+        corr_copy(k).start()
 
     crx[block_t, z] = ctx[...]
 
@@ -573,10 +616,14 @@
     for t in range(1, blocks):
         worst = jnp.maximum(worst, crx[t])
     for h in range(tiles):
-        tile = worst[h * per_tile]
-        for q in range(1, per_tile):
-            tile = jnp.where(lane_group == q, pltpu.roll(worst[h * per_tile + q], q * epd, 1), tile)
-        corr_out[:, h * LANES : (h + 1) * LANES] = tile[0:ITERS]
+        for k in range(ITERS):
+            tile = None
+            for q in range(per_tile):
+                r = (q - k) % per_tile
+                v = worst[h * per_tile + q]
+                v = v if r == 0 else pltpu.roll(v, r * epd, 1)
+                tile = v if tile is None else jnp.where(lane_group == q, v, tile)
+            corr_out[k : k + 1, h * LANES : (h + 1) * LANES] = tile
 
     @pl.loop(0, nz)
     def _(k):
@@ -594,7 +641,7 @@
             out_copy(k).wait_send()
 
     drain_blocks(first_copy)
-    for k in range(ITERS):
+    for k in range(ITERS + 1):
         drain_blocks(functools.partial(sweep_copy, k))
 
 
@@ -614,6 +661,7 @@
     both = vm((HS, epd, lanes), F32)
     thin = vm((HS, 1, lanes), F32)
     deep = DEPTH + epd
+    levels = slices.bit_length() - 1
     prm = [p.reshape(1, DOF) for p in (stiffness, damping, gravity, contact_stiffness, contact_damping)]
     states, corrections = pl.pallas_call(
         functools.partial(kernel, tm, env),
@@ -621,26 +669,28 @@
             jax.ShapeDtypeStruct((STATE, HS, env_local), F32),
             jax.ShapeDtypeStruct((ITERS, env_local), F32),
         ),
-        in_specs=[vmem] * 9,
+        in_specs=[pl.BlockSpec(memory_space=pl.ANY)] * 9,
         out_specs=(vmem, vmem),
         scratch_shapes=[
+            vm(init_state.shape, F32), vm((DOF, 2 * HS, env_local), F32), vm(contact.shape, jnp.int32),
+            vm((DOF, HS, DOF), F32), *[vm((1, DOF), F32)] * 5,
             vm((nz, ROWS_IN, LANES), F32), vm((nz, ROWS_IN, LANES), F32),
-            vm((8, LANES), F32), vm((nz, env, 8, LANES), F32),
+            vm((1, LANES), F32), vm((nz, env, 1, LANES), F32),
             vm((2 * HS, 40, env_local), F32), vm((env_local, LANES), F32),
             both, both, both, vm((1, lanes), F32), thin, thin,
-            vm((groups, WIDE, WIDE), BF16), vm((LANES, LANES), F32),
+            vm((groups, WIDE, WIDE), BF16), vm((groups, LANES, LANES), F32), vm((LANES, LANES), F32),
             vm((epd, lanes), F32), vm((epd, lanes), F32),
             vm((deep, lanes), F32), vm((deep, lanes), F32),
-            vm((slices, WIDE, WIDE), BF16), vm((slices, WIDE, WIDE), BF16),
-            vm((slices, WIDE, WIDE), BF16), vm((blocks, WIDE, WIDE), BF16),
-            vm((LANES, LANES), F32),
+            vm((levels * slices // 2, WIDE, WIDE), BF16),
+            vm((slices, WIDE, WIDE), BF16), vm((2 * blocks, WIDE, WIDE), BF16),
+            vm((deep, LANES), F32),
             vm((slices + 1, epd, LANES), F32), vm((slices, epd, LANES), F32),
-            vm((deep, LANES), F32), vm((blocks, deep, LANES), F32),
-            vm((ITERS, epd, LANES), F32), vm((ITERS, blocks, epd, LANES), F32),
+            vm((DEPTH, LANES), F32), vm((blocks, DEPTH, LANES), F32),
+            vm((ITERS + 1, epd, LANES), F32), vm((ITERS + 1, blocks, epd, LANES), F32),
             vm((nz, ROWS_OUT, LANES), F32), vm((nz, ROWS_OUT, LANES), F32),
-            vm((8, LANES), F32), vm((blocks, nz, 8, LANES), F32),
-            dma((nz,)), dma((nz,)), dma((nz, env)), dma((nz, env)),
-            dma((blocks,)), dma((blocks,)), dma((ITERS, blocks)), dma((ITERS, blocks)),
+            vm((1, LANES), F32), vm((blocks, nz, 1, LANES), F32),
+            dma((9,)), dma((nz,)), dma((nz,)), dma((nz, env)), dma((nz, env)),
+            dma((blocks,)), dma((blocks,)), dma((ITERS + 1, blocks)), dma((ITERS + 1, blocks)),
             dma((nz,)), dma((nz,)), dma((tm,)), dma((tm,)),
         ],
         compiler_params=pltpu.CompilerParams(collective_id=0, has_side_effects=True),

time: 96 us -> 83 us (0.86)
  the two profiles are of different devices: /device:TPU:39 before, /device:TPU:1 now
where the time goes in v2:
time: 83 us; the launch traced here: 82.9 us
  Pallas kernels  80.1 us (97%)
  local copies, waits for them, and re-layouts  2.17 us (3%)
    pallas_call x1, Pallas kernels, body(): pl.pallas_call(functools.partial(kernel, tm, env), out_shape=(jax.ShapeDt...  80.1 us
    unnamed x4, local copies, waits for them, and re-layouts  2.17 us

profile of v2, /device:TPU:1, one launch (start us, length us, event | category | flops | bytes accessed | tf_op | source)
XLA Modules:
  0.0 82.9 jit_solution(16753743775324841667)
XLA Ops:
  0.6 80.1 %parareal.1 = (f32[70,2,256]{2,1,0:T(2,128)}, f32[3,256]{1,0:T(4,128)}) custom-call(f32[70,256]{1,0:T(8,128)} %init_hbm.1, f32[35,4,256]{2,1,0:T(4,128)} %bitcast.9, s32[4,256]{1,0:T(4,128)} %contact_hbm.1, f32[35,2,35]{2,1,0:T(2,128)} %bitcast.10, f32[1,35]{1,0:T(1,128)} %bitcast.11, f32[1,35]{1,0:T(1,128)} %bitcast.12, f32[1,35]{1,0:T(1,128)} %bitcast.13, ...), custom_call_target="tpu_custom_call" | custom-call | tf_op jit(solution)/shard_map/parareal/pallas_call | solution.py:666
  80.7 0.0 copy-start
  80.7 1.6 %copy.13 = f32[2,70,256]{2,0,1:T(2,128)} copy(f32[2,70,256]{2,0,1:T(2,128)} %bitcast.8) | data formatting | bytes 286720
  82.3 0.0 copy-done
  82.3 0.6 copy.14
Async XLA Ops:
  80.7 1.6 %copy-start = (f32[3,256]{1,0:T(4,128)S(1)}, f32[3,256]{1,0:T(4,128)}, u32[]{:S(2)}) copy-start(f32[3,256]{1,0:T(4,128)} %get-tuple-element.9) | copy-start | bytes 9220

commit v3 on v2

--- a/solution.py
+++ b/solution.py
@@ -31,9 +31,9 @@
     -76.58010048603072, 41.205394649903326, -12.271261959178284,
 )
 
-ROWS_IN = 56
+ROWS_IN = 40
+ROWS_MAT = 16
 FOLD = 36
-KEEP = 80
 ROWS_OUT = 40
 DEPTH = 72
 
@@ -70,16 +70,17 @@
 
 
 class Plan:
-    def __init__(self, slices):
-        per = LANES // DOF
+    def __init__(self, sources):
+        self.per = LANES // DOF
         self.groups = []
-        self.where = []
-        for first in range(0, slices, per):
-            count = min(per, slices - first)
-            base = len(self.groups) * LANES
-            self.groups.append((base, first, count))
-            for pos in range(count):
-                self.where.append(base + pos * DOF)
+        self.slot = {}
+        for first in range(0, sources, self.per):
+            members = range(first, min(first + self.per, sources))
+            for a in range(HS):
+                for pos, i in enumerate(members):
+                    self.slot[HS * i + a] = (len(self.groups), pos)
+                self.groups.append((len(self.groups) * LANES, members, a))
+        self.where = [self.slot[n][0] * LANES + self.slot[n][1] * DOF for n in range(HS * sources)]
         self.lanes = len(self.groups) * LANES
 
 
@@ -88,11 +89,11 @@
     init_hbm, torque_hbm, contact_hbm, minv_hbm, stiff_hbm, damp_hbm, gravity_hbm, cstiff_hbm, cdamp_hbm,
     out, corr_out,
     init, torque, contact, minv, stiff, damp, gravity, cstiff, cdamp,
-    tx, rx, rowtx, rows, raw, inits,
-    tq, spring, fric, grav, cspring, cfric, wgt, stage, wtmp, ybuf, ubuf, ly, lu,
+    tx, rx, mtx, mrx, rowtx, rows, raw, inits,
+    tstage, gains, tq, spring, fric, grav, cspring, cfric, wgt, stage, wtmp, ybuf, ubuf, ly, lu,
     cmap, qmap, bmap, ctmp, xs, ends_buf,
     btx, brx, stx, srx, otx, orx, ctx, crx,
-    lsem, tsend, trecv, rsend, rrecv, bsend, brecv, ssend, srecv, osend, orecv, csend, crecv,
+    lsem, tsend, trecv, msend, mrecv, rsend, rrecv, bsend, brecv, ssend, srecv, osend, orecv, csend, crecv,
 ):
     pairs = (
         (torque_hbm, torque), (contact_hbm, contact), (minv_hbm, minv), (init_hbm, init), (stiff_hbm, stiff),
@@ -110,7 +111,7 @@
     slices = HS * nz
     per_tile = LANES // epd
     tiles = env_local // LANES
-    plan = Plan(slices)
+    plan = Plan(nz)
     me_t = lax.axis_index("tm")
     me_e = lax.axis_index("env")
     x = me_t // line
@@ -131,7 +132,7 @@
     def block_index(t):
         return t // CORES * line + z * CORES + lax.rem(t, CORES)
 
-    @pl.loop(1, tm)
+    @pl.loop(1, tm, unroll=True)
     def _(k):
         pl.semaphore_signal(
             barrier, inc=1, device_id={"tm": lax.rem(me_t + k, tm), "env": me_e}, device_id_type=MESH
@@ -164,7 +165,7 @@
     lower = lane_of <= row_of
     packed = jnp.where(lower, wtmp[0:40, :], pltpu.roll(wtmp[40:80, :], 1, 1))
     last = jnp.concatenate([packed[32:40], jnp.zeros((8, LANES), F32)], axis=0)
-    mtx = packed[0:16] + pltpu.roll(packed[16:32], FOLD, 1) + pltpu.roll(last, 2 * FOLD, 1)
+    mtx[...] = packed[0:16] + pltpu.roll(packed[16:32], FOLD, 1) + pltpu.roll(last, 2 * FOLD, 1)
     for h in range(tiles):
         rolled = {}
         for k in range(2 * HS):
@@ -175,8 +176,7 @@
             acc = rolled[0, (0 - q) % per_tile]
             for k in range(1, 2 * HS):
                 acc = jnp.where(lane_group == k, rolled[k, (k - q) % per_tile], acc)
-            tx[h * per_tile + q, 0:40, :] = acc
-            tx[h * per_tile + q, 40:ROWS_IN, :] = mtx
+            tx[h * per_tile + q] = acc
     totals = jnp.sum(hits, axis=1, keepdims=True)
     row = jnp.broadcast_to(totals[0:1], (1, LANES))
     for k in range(1, 2 * HS):
@@ -205,6 +205,26 @@
             device_id_type=MESH,
         )
 
+    def mat_copy(k):
+        return pltpu.make_async_remote_copy(
+            src_ref=mtx,
+            dst_ref=mrx.at[my_source],
+            send_sem=msend.at[k],
+            recv_sem=mrecv.at[my_source],
+            device_id={"tm": dest_index(k), "env": me_e},
+            device_id_type=MESH,
+        )
+
+    def mat_arrival(i):
+        return pltpu.make_async_remote_copy(
+            src_ref=mtx,
+            dst_ref=mrx.at[i],
+            send_sem=msend.at[0],
+            recv_sem=mrecv.at[i],
+            device_id={"tm": dest_index(0), "env": me_e},
+            device_id_type=MESH,
+        )
+
     def row_copy(k, r):
         return pltpu.make_async_remote_copy(
             src_ref=rowtx,
@@ -241,14 +261,17 @@
         def _(r):
             row_copy(k, r).start()
 
-    for k in sorted(range(nz), key=lambda k: -min(k, nz - k)):
-        @pl.when(other(k))
-        def _(k=k):
-            in_copy(k).start()
+    far_first = sorted(range(nz), key=lambda k: -min(k, nz - k))
+    for make in (mat_copy, in_copy):
+        for k in far_first:
+            @pl.when(other(k))
+            def _(k=k, make=make):
+                make(k).start()
 
     @pl.when(own_here)
     def _():
         rx[my_source] = tx[z]
+        mrx[my_source] = mtx[...]
         rows[my_source, me_e] = rowtx[...]
 
     ratio = float(SUB)
@@ -257,77 +280,74 @@
     scale = jnp.where(lane_of < DOF, TWO_PI, to_u)
     shrink = jnp.where(lane_of < DOF, 1.0 / TWO_PI, 1.0 / to_u)
 
-    for ref in (tq, spring, fric, grav, cspring, cfric, ybuf, ubuf, ly, lu, ctmp, stage, wgt, cmap, qmap, bmap):
+    for ref in (tstage, gains, tq, spring, fric, grav, cspring, cfric, ybuf, ubuf, ly, lu, ctmp, stage, wgt, cmap, qmap, bmap):
         clear(ref)
     for h in range(tiles):
         inits[h * LANES : (h + 1) * LANES, :] = (
             pad_rows(init[:, h * LANES : (h + 1) * LANES], LANES).T * shrink
         )
     start_state = inits[pl.ds(pl.multiple_of(z * epd, epd), epd), :]
-    deep = DEPTH + epd
     first_start = jnp.where(block_t == 0, start_state, 0.0)
-    rank = lax.broadcasted_iota(jnp.int32, (deep, DOF), 0)
-    col = lax.broadcasted_iota(jnp.int32, (deep, DOF), 1)
+    rank = lax.broadcasted_iota(jnp.int32, (DEPTH, DOF), 0)
+    col = lax.broadcasted_iota(jnp.int32, (DEPTH, DOF), 1)
     for n in range(slices):
         cut = pl.ds(plan.where[n], DOF)
         ly[:, cut] = jnp.where(rank == col, 1.0, 0.0)
         lu[:, cut] = jnp.where(rank == col + DOF, 1.0, 0.0)
-        grav[:, cut] = jnp.broadcast_to(gravity, (1, DOF))
-    ly[DEPTH:, 0:DOF] = first_start[:, 0:DOF]
-    lu[DEPTH:, 0:DOF] = first_start[:, DOF : 2 * DOF]
+        grav[:, cut] = gravity
+        gains[0, :, cut] = TWO_PI * stiff
+        gains[1, :, cut] = TWO_PI * cstiff
+        gains[2, :, cut] = to_u * damp
+        gains[3, :, cut] = to_u * cdamp
+    ybuf[:, 0:DOF] = first_start[:, 0:DOF]
+    ubuf[:, 0:DOF] = first_start[:, DOF : 2 * DOF]
 
     square_row = lax.broadcasted_iota(jnp.int32, (40, LANES), 0)
     for i in range(nz):
         @pl.when(other_source(i))
         def _(i=i):
-            in_arrival(i).wait_recv()
+            mat_arrival(i).wait_recv()
             row_arrival(i, 0).wait_recv()
 
         @pl.loop(1, ny)
         def _(r, i=i):
             row_arrival(i, r).wait_recv()
 
-        folded = rx[i, 40:ROWS_IN, :]
+        folded = mrx[i]
         square = jnp.concatenate(
             [folded, pltpu.roll(folded, LANES - FOLD, 1), pltpu.roll(folded[0:8], LANES - 2 * FOLD, 1)], axis=0
         )
         shifted = pltpu.roll(square, LANES - 1, 1)
-        turned = jnp.concatenate([rx[i, 0:40, :], square, shifted, jnp.zeros((8, LANES), F32)], axis=0).T
+        turned = pad_rows(jnp.concatenate([square, shifted], axis=0), LANES).T
         matrices = (
-            jnp.where(lane_of <= square_row, square, pltpu.roll(turned[0:40], LANES - 40, 1)),
-            jnp.where(lane_of >= square_row, shifted, pltpu.roll(turned[0:40], LANES - 80, 1)),
+            jnp.where(lane_of <= square_row, square, turned[0:40]),
+            jnp.where(lane_of >= square_row, shifted, pltpu.roll(turned[0:40], LANES - 40, 1)),
         )
         means = jnp.sum(rows[i], axis=0) * (1.0 / (env_local * ny))
         for a in range(HS):
             n = HS * i + a
             cut = pl.ds(plan.where[n], DOF)
-            g, pos = divmod(n, LANES // DOF)
+            g, pos = plan.slot[n]
             stage[g, pl.ds(pos * DOF, DOF), pl.ds(pos * DOF, DOF)] = (
                 fine_dt * fine_dt / TWO_PI
             ) * matrices[a][0:DOF, 0:DOF]
             for j in range(HS):
                 k = a * HS + j
-                piece = turned[k * epd : (k + 1) * epd, :]
-                hit = piece[:, DOF : DOF + 1]
                 mean = means[:, k * epd : k * epd + 1]
-                tq[j, :, cut] = piece[:, 0:DOF]
-                spring[j, :, cut] = TWO_PI * (stiff + hit * cstiff)
-                fric[j, :, cut] = to_u * (damp + hit * cdamp)
                 cspring[j, :, cut] = TWO_PI * (stiff + gravity + mean * cstiff)
                 cfric[j, :, cut] = to_u * (damp + mean * cdamp)
 
-    for g, (base, first, count) in enumerate(plan.groups):
+    for g, (base, members, a) in enumerate(plan.groups):
         put(wgt, g, stage[g])
 
     def product(force, g):
         return through(force, wgt[g])
 
-    for g, (base, first, count) in enumerate(plan.groups):
+    for g, (base, members, a) in enumerate(plan.groups):
         cut = pl.ds(base, LANES)
         y, u = ly[:, cut], lu[:, cut]
         for j in range(HS):
-            push = jnp.concatenate([jnp.zeros((DEPTH, LANES), F32), tq[j, :, cut]], axis=0)
-            force = push - cspring[j, :, cut] * y - cfric[j, :, cut] * u
+            force = -cspring[j, :, cut] * y - cfric[j, :, cut] * u
             u = u + ratio * product(force, g)
             y = y + ratio * u
         ly[:, cut] = y
@@ -345,24 +365,22 @@
         place = 0
         for m in range(0, slices, 2 * step):
             for i in range(step):
-                yield place, m + step - 1, m + step + i
+                yield level * (slices // 2) + place, m + step - 1, m + step + i
                 place += 1
 
-    keep_offsets = lax.broadcasted_iota(jnp.int32, (deep, LANES), 0) >= DEPTH
     for level in range(levels):
         for place, left, n in right_half(level):
-            put(cmap, level * (slices // 2) + place, stacks[n][0:DEPTH])
+            put(cmap, place, stacks[n])
         for place, left, n in right_half(level):
-            moved = through(stacks[left], cmap[level * (slices // 2) + place])
-            stacks[n] = moved + jnp.where(keep_offsets, stacks[n], 0.0)
+            stacks[n] = through(stacks[left], cmap[place])
+    btx[...] = stacks[slices - 1]
     for n in range(slices):
-        put(qmap, n, stacks[n][0:DEPTH])
-    ends = [stack[DEPTH:] for stack in stacks]
+        put(qmap, n, stacks[n])
 
     def sweep(ends):
         for level in range(levels):
             for place, left, n in right_half(level):
-                ends[n] = ends[n] + through(ends[left], cmap[level * (slices // 2) + place])
+                ends[n] = ends[n] + through(ends[left], cmap[place])
 
     def first_copy(d):
         return pltpu.make_async_remote_copy(
@@ -425,13 +443,60 @@
             def _():
                 copy(d).wait_send()
 
-    btx[...] = stacks[slices - 1][0:DEPTH]
+    @pl.when(block_t > 0)
+    def _():
+        send_blocks(first_copy)
+
+    mark = plan.per * DOF
+    for part in range(0, nz, plan.per):
+        for pos, i in enumerate(range(part, min(part + plan.per, nz))):
+            @pl.when(other_source(i))
+            def _(i=i):
+                in_arrival(i).wait_recv()
+
+            tstage[part // plan.per, pos * DOF : (pos + 1) * DOF, :] = rx[i, 0:DOF, :]
+            tstage[part // plan.per, mark + pos : mark + pos + 1, :] = rx[i, DOF : DOF + 1, :]
+        turned = tstage[part // plan.per].T
+        for a in range(HS):
+            base = (part // plan.per * HS + a) * LANES
+            cut = pl.ds(base, LANES)
+            for j in range(HS):
+                k = a * HS + j
+                piece = turned[k * epd : (k + 1) * epd, :]
+                hit = piece[:, mark : mark + 1]
+                for pos in range(1, plan.per):
+                    hit = jnp.where(lane_of >= pos * DOF, piece[:, mark + pos : mark + pos + 1], hit)
+                tq[j, :, cut] = jnp.where(lane_of < mark, piece, 0.0)
+                spring[j, :, cut] = gains[0, :, cut] + hit * gains[1, :, cut]
+                fric[j, :, cut] = gains[2, :, cut] + hit * gains[3, :, cut]
+
+    for g, (base, members, a) in enumerate(plan.groups):
+        cut = pl.ds(base, LANES)
+        y, u = ybuf[:, cut], ubuf[:, cut]
+        for j in range(HS):
+            force = tq[j, :, cut] - cspring[j, :, cut] * y - cfric[j, :, cut] * u
+            u = u + ratio * product(force, g)
+            y = y + ratio * u
+        ybuf[:, cut] = y
+        ubuf[:, cut] = u
+
+    def packed_state(n):
+        cut = pl.ds(plan.where[n], DOF)
+        zero = jnp.zeros((epd, LANES - 2 * DOF), F32)
+        return jnp.concatenate([ybuf[:, cut], ubuf[:, cut], zero], axis=1)
+
+    ends = [packed_state(n) for n in range(slices)]
+    sweep(ends)
     stx[0] = ends[slices - 1]
     for n in range(slices):
         ends_buf[n] = ends[n]
-    send_blocks(first_copy)
     send_blocks(functools.partial(sweep_copy, 0))
-    await_blocks(first_arrival)
+    @pl.loop(1, blocks)
+    def _(d):
+        @pl.when(block_t - d > 0)
+        def _():
+            first_arrival(d).wait_recv()
+
     eye = jnp.where(
         lax.broadcasted_iota(jnp.int32, (DEPTH, LANES), 0) == lane_of, 1.0, 0.0
     )
@@ -482,7 +547,7 @@
 
             def substep(counter, carry):
                 result = []
-                for g, (base, first, count) in enumerate(plan.groups):
+                for g, (base, members, a) in enumerate(plan.groups):
                     y, u = carry[g]
                     cut = pl.ds(base, LANES)
                     t = y - jnp.round(y)
@@ -502,18 +567,14 @@
 
             first_state = tuple(
                 (ybuf[:, pl.ds(base, LANES)], ubuf[:, pl.ds(base, LANES)])
-                for base, first, count in plan.groups
+                for base, members, a in plan.groups
             )
             last = lax.fori_loop(0, SUB, substep, first_state, unroll=UNROLL)
-            for g, (base, first, count) in enumerate(plan.groups):
+            for g, (base, members, a) in enumerate(plan.groups):
                 ybuf[:, pl.ds(base, LANES)] = last[g][0]
                 ubuf[:, pl.ds(base, LANES)] = last[g][1]
 
-        zero = jnp.zeros((epd, LANES - 2 * DOF), F32)
-        ends = []
-        for n in range(slices):
-            cut = pl.ds(plan.where[n], DOF)
-            ends.append(jnp.concatenate([ybuf[:, cut], ubuf[:, cut], zero], axis=1) - xs[n + 1])
+        ends = [packed_state(n) - xs[n + 1] for n in range(slices)]
         sweep(ends)
         stx[k + 1] = ends[slices - 1]
         for n in range(slices):
@@ -575,15 +636,15 @@
             device_id_type=MESH,
         )
 
+    @pl.loop(1, tm, unroll=True)
+    def _(k):
+        corr_copy(k).start()
+
     @pl.loop(0, nz)
     def _(i):
         @pl.when(other_source(i))
         def _():
             out_copy(i).start()
-
-    @pl.loop(1, tm)
-    def _(k):
-        corr_copy(k).start()
 
     crx[block_t, z] = ctx[...]
 
@@ -608,7 +669,7 @@
                 tile = v if tile is None else jnp.where(lane_group == q, v, tile)
             out[half_state * DOF : half_state * DOF + DOF, a, h * LANES : (h + 1) * LANES] = tile[0:DOF]
 
-    @pl.loop(1, tm)
+    @pl.loop(1, tm, unroll=True)
     def _(k):
         corr_copy(k).wait()
 
@@ -630,6 +691,7 @@
         @pl.when(other(k))
         def _():
             in_copy(k).wait_send()
+            mat_copy(k).wait_send()
             row_copy(k, 0).wait_send()
 
         @pl.loop(1, ny)
@@ -640,7 +702,10 @@
         def _():
             out_copy(k).wait_send()
 
-    drain_blocks(first_copy)
+    @pl.when(block_t > 0)
+    def _():
+        drain_blocks(first_copy)
+
     for k in range(ITERS + 1):
         drain_blocks(functools.partial(sweep_copy, k))
 
@@ -652,7 +717,7 @@
     epd = env_local // nz
     slices = HS * nz
     blocks = tm // (nz * CORES) * CORES
-    plan = Plan(slices)
+    plan = Plan(nz)
     groups = len(plan.groups)
     lanes = plan.lanes
     vm = pltpu.VMEM
@@ -660,7 +725,6 @@
     vmem = pl.BlockSpec(memory_space=pltpu.VMEM)
     both = vm((HS, epd, lanes), F32)
     thin = vm((HS, 1, lanes), F32)
-    deep = DEPTH + epd
     levels = slices.bit_length() - 1
     prm = [p.reshape(1, DOF) for p in (stiffness, damping, gravity, contact_stiffness, contact_damping)]
     states, corrections = pl.pallas_call(
@@ -675,21 +739,23 @@
             vm(init_state.shape, F32), vm((DOF, 2 * HS, env_local), F32), vm(contact.shape, jnp.int32),
             vm((DOF, HS, DOF), F32), *[vm((1, DOF), F32)] * 5,
             vm((nz, ROWS_IN, LANES), F32), vm((nz, ROWS_IN, LANES), F32),
+            vm((ROWS_MAT, LANES), F32), vm((nz, ROWS_MAT, LANES), F32),
             vm((1, LANES), F32), vm((nz, env, 1, LANES), F32),
             vm((2 * HS, 40, env_local), F32), vm((env_local, LANES), F32),
+            vm((-(-nz // plan.per), LANES, LANES), F32), vm((4, 1, lanes), F32),
             both, both, both, vm((1, lanes), F32), thin, thin,
             vm((groups, WIDE, WIDE), BF16), vm((groups, LANES, LANES), F32), vm((LANES, LANES), F32),
             vm((epd, lanes), F32), vm((epd, lanes), F32),
-            vm((deep, lanes), F32), vm((deep, lanes), F32),
+            vm((DEPTH, lanes), F32), vm((DEPTH, lanes), F32),
             vm((levels * slices // 2, WIDE, WIDE), BF16),
             vm((slices, WIDE, WIDE), BF16), vm((2 * blocks, WIDE, WIDE), BF16),
-            vm((deep, LANES), F32),
+            vm((DEPTH, LANES), F32),
             vm((slices + 1, epd, LANES), F32), vm((slices, epd, LANES), F32),
             vm((DEPTH, LANES), F32), vm((blocks, DEPTH, LANES), F32),
             vm((ITERS + 1, epd, LANES), F32), vm((ITERS + 1, blocks, epd, LANES), F32),
             vm((nz, ROWS_OUT, LANES), F32), vm((nz, ROWS_OUT, LANES), F32),
             vm((1, LANES), F32), vm((blocks, nz, 1, LANES), F32),
-            dma((9,)), dma((nz,)), dma((nz,)), dma((nz, env)), dma((nz, env)),
+            dma((9,)), dma((nz,)), dma((nz,)), dma((nz,)), dma((nz,)), dma((nz, env)), dma((nz, env)),
             dma((blocks,)), dma((blocks,)), dma((ITERS + 1, blocks)), dma((ITERS + 1, blocks)),
             dma((nz,)), dma((nz,)), dma((tm,)), dma((tm,)),
         ],

time: 83 us -> 78.2 us (0.942)
  Pallas kernels: 80.1 us -> 75.3 us
    pallas_call x1, Pallas kernels: 80.1 us -> 75.3 us  [body(): pl.pallas_call(functools.partial(kernel, tm, env), out_shape=(jax.ShapeDt...]
where the time goes in v3:
time: 78.2 us; the launch traced here: 78.1 us
  Pallas kernels  75.3 us (96%)
  local copies, waits for them, and re-layouts  2.17 us (3%)
    pallas_call x1, Pallas kernels, body(): pl.pallas_call(functools.partial(kernel, tm, env), out_shape=(jax.ShapeDt...  75.3 us
    unnamed x4, local copies, waits for them, and re-layouts  2.17 us

profile of v3, /device:TPU:1, one launch (start us, length us, event | category | flops | bytes accessed | tf_op | source)
XLA Modules:
  0.0 78.1 jit_solution(7348876542616434149)
XLA Ops:
  0.6 75.3 %parareal.1 = (f32[70,2,256]{2,1,0:T(2,128)}, f32[3,256]{1,0:T(4,128)}) custom-call(f32[70,256]{1,0:T(8,128)} %init_hbm.1, f32[35,4,256]{2,1,0:T(4,128)} %bitcast.9, s32[4,256]{1,0:T(4,128)} %contact_hbm.1, f32[35,2,35]{2,1,0:T(2,128)} %bitcast.10, f32[1,35]{1,0:T(1,128)} %bitcast.11, f32[1,35]{1,0:T(1,128)} %bitcast.12, f32[1,35]{1,0:T(1,128)} %bitcast.13, ...), custom_call_target="tpu_custom_call" | custom-call | tf_op jit(solution)/shard_map/parareal/pallas_call | solution.py:730
  75.9 0.0 copy-start
  75.9 1.6 %copy.13 = f32[2,70,256]{2,0,1:T(2,128)} copy(f32[2,70,256]{2,0,1:T(2,128)} %bitcast.8) | data formatting | bytes 286720
  77.5 0.0 copy-done
  77.5 0.6 copy.14
Async XLA Ops:
  75.9 1.6 %copy-start = (f32[3,256]{1,0:T(4,128)S(1)}, f32[3,256]{1,0:T(4,128)}, u32[]{:S(2)}) copy-start(f32[3,256]{1,0:T(4,128)} %get-tuple-element.9) | copy-start | bytes 9220

commit v4 on v3

--- a/solution.py
+++ b/solution.py
@@ -36,6 +36,7 @@
 FOLD = 36
 ROWS_OUT = 40
 DEPTH = 72
+ROWS_MAP = 48
 
 
 def split(value):
@@ -67,6 +68,21 @@
 
 def pad_rows(value, rows):
     return jnp.concatenate([value, jnp.zeros((rows - value.shape[0], value.shape[1]), F32)], axis=0)
+
+
+def fold_map(value, lane_of):
+    value = jnp.where(lane_of < DOF, value, 0.0), jnp.where(lane_of < DOF, pltpu.roll(value, LANES - DOF, 1), 0.0)
+    tall = jnp.concatenate(value, axis=0)
+    first, second, third = (tall[r : r + ROWS_MAP] for r in range(0, 2 * DEPTH, ROWS_MAP))
+    return first + pltpu.roll(second, DOF, 1) + pltpu.roll(third, 2 * DOF, 1)
+
+
+def unfold_map(value, lane_of):
+    tall = jnp.concatenate(
+        [value, pltpu.roll(value, LANES - DOF, 1), pltpu.roll(value, LANES - 2 * DOF, 1)], axis=0
+    )
+    right = jnp.where(lane_of < 2 * DOF, pltpu.roll(tall[DEPTH:], DOF, 1), 0.0)
+    return jnp.where(lane_of < DOF, tall[0:DEPTH], right)
 
 
 class Plan:
@@ -100,8 +116,6 @@
         (damp_hbm, damp), (gravity_hbm, gravity), (cstiff_hbm, cstiff), (cdamp_hbm, cdamp),
     )
     local = [pltpu.make_async_copy(src, dst, lsem.at[i]) for i, (src, dst) in enumerate(pairs)]
-    for copy in local:
-        copy.start()
     nz = NZ
     half = nz // 2
     line = nz * CORES
@@ -138,9 +152,12 @@
             barrier, inc=1, device_id={"tm": lax.rem(me_t + k, tm), "env": me_e}, device_id_type=MESH
         )
 
+    for copy in local:
+        copy.start()
+
     @pl.loop(1, ny)
     def _(r):
-        @pl.loop(0, nz)
+        @pl.loop(0, nz, unroll=True)
         def _(i):
             pl.semaphore_signal(
                 barrier, inc=1,
@@ -178,10 +195,11 @@
                 acc = jnp.where(lane_group == k, rolled[k, (k - q) % per_tile], acc)
             tx[h * per_tile + q] = acc
     totals = jnp.sum(hits, axis=1, keepdims=True)
-    row = jnp.broadcast_to(totals[0:1], (1, LANES))
-    for k in range(1, 2 * HS):
-        row = jnp.where(lane_group == k, jnp.broadcast_to(totals[k : k + 1], (1, LANES)), row)
+    row = jnp.zeros((1, LANES), F32)
+    for k in range(2 * HS):
+        row = jnp.where(lane_of == 3 * FOLD + k, jnp.broadcast_to(totals[k : k + 1], (1, LANES)), row)
     rowtx[...] = row
+    mtx[0:1, :] = mtx[0:1, :] + row
 
     pl.semaphore_wait(barrier, tm - 1 + (ny - 1) * nz)
 
@@ -228,20 +246,20 @@
     def row_copy(k, r):
         return pltpu.make_async_remote_copy(
             src_ref=rowtx,
-            dst_ref=rows.at[my_source, me_e],
-            send_sem=rsend.at[k, r],
-            recv_sem=rrecv.at[my_source, r],
+            dst_ref=rows.at[r, my_source],
+            send_sem=rsend.at[0],
+            recv_sem=rrecv.at[0],
             device_id={"tm": dest_index(k), "env": lax.rem(me_e + r, ny)},
             device_id_type=MESH,
         )
 
-    def row_arrival(i, r):
-        return pltpu.make_async_remote_copy(
-            src_ref=rowtx,
-            dst_ref=rows.at[i, lax.rem(me_e - r + ny, ny)],
-            send_sem=rsend.at[0, r],
-            recv_sem=rrecv.at[i, r],
-            device_id={"tm": dest_index(0), "env": lax.rem(me_e + r, ny)},
+    def rows_all():
+        return pltpu.make_async_remote_copy(
+            src_ref=rows.at[pl.ds(1, ny - 1)],
+            dst_ref=rows.at[pl.ds(1, ny - 1)],
+            send_sem=rsend.at[0],
+            recv_sem=rrecv.at[0],
+            device_id={"tm": dest_index(0), "env": lax.rem(me_e + 1, ny)},
             device_id_type=MESH,
         )
 
@@ -251,16 +269,9 @@
     def other_source(i):
         return jnp.logical_not(jnp.logical_and(own_here, i == my_source))
 
-    @pl.loop(0, nz)
-    def _(k):
-        @pl.when(other(k))
-        def _():
-            row_copy(k, 0).start()
-
-        @pl.loop(1, ny)
-        def _(r):
+    for r in range(1, ny):
+        for k in range(nz):
             row_copy(k, r).start()
-
     far_first = sorted(range(nz), key=lambda k: -min(k, nz - k))
     for make in (mat_copy, in_copy):
         for k in far_first:
@@ -272,7 +283,6 @@
     def _():
         rx[my_source] = tx[z]
         mrx[my_source] = mtx[...]
-        rows[my_source, me_e] = rowtx[...]
 
     ratio = float(SUB)
     stiff, damp, gravity, cstiff, cdamp = (r[...] for r in (stiff, damp, gravity, cstiff, cdamp))
@@ -299,6 +309,7 @@
         gains[1, :, cut] = TWO_PI * cstiff
         gains[2, :, cut] = to_u * damp
         gains[3, :, cut] = to_u * cdamp
+        gains[4, :, cut] = TWO_PI * gravity
     ybuf[:, 0:DOF] = first_start[:, 0:DOF]
     ubuf[:, 0:DOF] = first_start[:, DOF : 2 * DOF]
 
@@ -307,11 +318,6 @@
         @pl.when(other_source(i))
         def _(i=i):
             mat_arrival(i).wait_recv()
-            row_arrival(i, 0).wait_recv()
-
-        @pl.loop(1, ny)
-        def _(r, i=i):
-            row_arrival(i, r).wait_recv()
 
         folded = mrx[i]
         square = jnp.concatenate(
@@ -323,7 +329,6 @@
             jnp.where(lane_of <= square_row, square, turned[0:40]),
             jnp.where(lane_of >= square_row, shifted, pltpu.roll(turned[0:40], LANES - 40, 1)),
         )
-        means = jnp.sum(rows[i], axis=0) * (1.0 / (env_local * ny))
         for a in range(HS):
             n = HS * i + a
             cut = pl.ds(plan.where[n], DOF)
@@ -331,17 +336,29 @@
             stage[g, pl.ds(pos * DOF, DOF), pl.ds(pos * DOF, DOF)] = (
                 fine_dt * fine_dt / TWO_PI
             ) * matrices[a][0:DOF, 0:DOF]
-            for j in range(HS):
-                k = a * HS + j
-                mean = means[:, k * epd : k * epd + 1]
-                cspring[j, :, cut] = TWO_PI * (stiff + gravity + mean * cstiff)
-                cfric[j, :, cut] = to_u * (damp + mean * cdamp)
-
     for g, (base, members, a) in enumerate(plan.groups):
         put(wgt, g, stage[g])
 
     def product(force, g):
         return through(force, wgt[g])
+
+    if ny > 1:
+        rows_all().wait_recv()
+    counts = []
+    for i in range(nz):
+        total = mrx[i, 0:1, :]
+        for r in range(1, ny):
+            total = total + rows[r, i]
+        counts.append(total * (1.0 / (env_local * ny)))
+    for base, members, a in plan.groups:
+        cut = pl.ds(base, LANES)
+        for j in range(HS):
+            spot = 3 * FOLD + a * HS + j
+            mean = counts[members[0]][:, spot : spot + 1]
+            for pos, i in enumerate(members):
+                mean = jnp.where(lane_of >= pos * DOF, counts[i][:, spot : spot + 1], mean)
+            cspring[j, :, cut] = gains[0, :, cut] + gains[4, :, cut] + mean * gains[1, :, cut]
+            cfric[j, :, cut] = gains[2, :, cut] + mean * gains[3, :, cut]
 
     for g, (base, members, a) in enumerate(plan.groups):
         cut = pl.ds(base, LANES)
@@ -362,25 +379,32 @@
 
     def right_half(level):
         step = 1 << level
-        place = 0
+        found = []
         for m in range(0, slices, 2 * step):
             for i in range(step):
-                yield level * (slices // 2) + place, m + step - 1, m + step + i
-                place += 1
+                found.append((level * (slices // 2) + len(found), m + step - 1, m + step + i))
+        if level == levels - 1:
+            found = found[-1:] + found[:-1]
+        return found
 
     for level in range(levels):
         for place, left, n in right_half(level):
             put(cmap, place, stacks[n])
         for place, left, n in right_half(level):
             stacks[n] = through(stacks[left], cmap[place])
-    btx[...] = stacks[slices - 1]
+    btx[...] = fold_map(stacks[slices - 1], lane_of)
     for n in range(slices):
         put(qmap, n, stacks[n])
 
-    def sweep(ends):
+    def sweep(ends, k):
         for level in range(levels):
             for place, left, n in right_half(level):
                 ends[n] = ends[n] + through(ends[left], cmap[place])
+                if n == slices - 1 and level == levels - 1:
+                    stx[k] = ends[n]
+                    send_blocks(functools.partial(sweep_copy, k))
+        for n in range(slices):
+            ends_buf[n] = ends[n]
 
     def first_copy(d):
         return pltpu.make_async_remote_copy(
@@ -486,11 +510,7 @@
         return jnp.concatenate([ybuf[:, cut], ubuf[:, cut], zero], axis=1)
 
     ends = [packed_state(n) for n in range(slices)]
-    sweep(ends)
-    stx[0] = ends[slices - 1]
-    for n in range(slices):
-        ends_buf[n] = ends[n]
-    send_blocks(functools.partial(sweep_copy, 0))
+    sweep(ends, 0)
     @pl.loop(1, blocks)
     def _(d):
         @pl.when(block_t - d > 0)
@@ -500,7 +520,7 @@
     eye = jnp.where(
         lax.broadcasted_iota(jnp.int32, (DEPTH, LANES), 0) == lane_of, 1.0, 0.0
     )
-    maps = {t: jnp.where(t < block_t, brx[t], eye) for t in range(1, blocks - 1)}
+    maps = {t: jnp.where(t < block_t, unfold_map(brx[t], lane_of), eye) for t in range(1, blocks - 1)}
     pieces = {(t, t): maps[t] for t in maps}
 
     def join(a, b, c):
@@ -575,11 +595,7 @@
                 ubuf[:, pl.ds(base, LANES)] = last[g][1]
 
         ends = [packed_state(n) - xs[n + 1] for n in range(slices)]
-        sweep(ends)
-        stx[k + 1] = ends[slices - 1]
-        for n in range(slices):
-            ends_buf[n] = ends[n]
-        send_blocks(functools.partial(sweep_copy, k + 1))
+        sweep(ends, k + 1)
         await_blocks(functools.partial(sweep_arrival, k + 1))
         entry = enter(k + 1)
         xs[0] = xs[0] + entry
@@ -629,9 +645,9 @@
     def corr_copy(k):
         return pltpu.make_async_remote_copy(
             src_ref=ctx,
-            dst_ref=crx.at[block_t, z],
-            send_sem=csend.at[k],
-            recv_sem=crecv.at[k],
+            dst_ref=crx.at[k],
+            send_sem=csend.at[0],
+            recv_sem=crecv.at[0],
             device_id={"tm": lax.rem(me_t + k, tm), "env": me_e},
             device_id_type=MESH,
         )
@@ -646,7 +662,7 @@
         def _():
             out_copy(i).start()
 
-    crx[block_t, z] = ctx[...]
+    crx[0] = ctx[...]
 
     @pl.when(own_here)
     def _():
@@ -669,13 +685,22 @@
                 tile = v if tile is None else jnp.where(lane_group == q, v, tile)
             out[half_state * DOF : half_state * DOF + DOF, a, h * LANES : (h + 1) * LANES] = tile[0:DOF]
 
-    @pl.loop(1, tm, unroll=True)
-    def _(k):
-        corr_copy(k).wait()
-
-    worst = crx[0]
-    for t in range(1, blocks):
-        worst = jnp.maximum(worst, crx[t])
+    pltpu.make_async_remote_copy(
+        src_ref=crx.at[pl.ds(1, tm - 1)],
+        dst_ref=crx.at[pl.ds(1, tm - 1)],
+        send_sem=csend.at[0],
+        recv_sem=crecv.at[0],
+        device_id={"tm": lax.rem(me_t + 1, tm), "env": me_e},
+        device_id_type=MESH,
+    ).wait()
+    worst = []
+    for p in range(nz):
+        most = None
+        for t in range(blocks):
+            sender = t // CORES * line + p * CORES + t % CORES
+            value = crx[lax.rem(me_t - sender + tm, tm)]
+            most = value if most is None else jnp.maximum(most, value)
+        worst.append(most)
     for h in range(tiles):
         for k in range(ITERS):
             tile = None
@@ -692,15 +717,13 @@
         def _():
             in_copy(k).wait_send()
             mat_copy(k).wait_send()
-            row_copy(k, 0).wait_send()
-
-        @pl.loop(1, ny)
-        def _(r):
-            row_copy(k, r).wait_send()
 
         @pl.when(other_source(k))
         def _():
             out_copy(k).wait_send()
+
+    if ny > 1:
+        rows_all().wait_send()
 
     @pl.when(block_t > 0)
     def _():
@@ -730,8 +753,8 @@
     states, corrections = pl.pallas_call(
         functools.partial(kernel, tm, env),
         out_shape=(
-            jax.ShapeDtypeStruct((STATE, HS, env_local), F32),
-            jax.ShapeDtypeStruct((ITERS, env_local), F32),
+            vm((STATE, HS, env_local), F32),
+            vm((ITERS, env_local), F32),
         ),
         in_specs=[pl.BlockSpec(memory_space=pl.ANY)] * 9,
         out_specs=(vmem, vmem),
@@ -740,9 +763,9 @@
             vm((DOF, HS, DOF), F32), *[vm((1, DOF), F32)] * 5,
             vm((nz, ROWS_IN, LANES), F32), vm((nz, ROWS_IN, LANES), F32),
             vm((ROWS_MAT, LANES), F32), vm((nz, ROWS_MAT, LANES), F32),
-            vm((1, LANES), F32), vm((nz, env, 1, LANES), F32),
+            vm((1, LANES), F32), vm((env, nz, 1, LANES), F32),
             vm((2 * HS, 40, env_local), F32), vm((env_local, LANES), F32),
-            vm((-(-nz // plan.per), LANES, LANES), F32), vm((4, 1, lanes), F32),
+            vm((-(-nz // plan.per), LANES, LANES), F32), vm((5, 1, lanes), F32),
             both, both, both, vm((1, lanes), F32), thin, thin,
             vm((groups, WIDE, WIDE), BF16), vm((groups, LANES, LANES), F32), vm((LANES, LANES), F32),
             vm((epd, lanes), F32), vm((epd, lanes), F32),
@@ -751,13 +774,13 @@
             vm((slices, WIDE, WIDE), BF16), vm((2 * blocks, WIDE, WIDE), BF16),
             vm((DEPTH, LANES), F32),
             vm((slices + 1, epd, LANES), F32), vm((slices, epd, LANES), F32),
-            vm((DEPTH, LANES), F32), vm((blocks, DEPTH, LANES), F32),
+            vm((ROWS_MAP, LANES), F32), vm((blocks, ROWS_MAP, LANES), F32),
             vm((ITERS + 1, epd, LANES), F32), vm((ITERS + 1, blocks, epd, LANES), F32),
             vm((nz, ROWS_OUT, LANES), F32), vm((nz, ROWS_OUT, LANES), F32),
-            vm((1, LANES), F32), vm((blocks, nz, 1, LANES), F32),
-            dma((9,)), dma((nz,)), dma((nz,)), dma((nz,)), dma((nz,)), dma((nz, env)), dma((nz, env)),
+            vm((1, LANES), F32), vm((tm, 1, LANES), F32),
+            dma((9,)), dma((nz,)), dma((nz,)), dma((nz,)), dma((nz,)), dma((1,)), dma((1,)),
             dma((blocks,)), dma((blocks,)), dma((ITERS + 1, blocks)), dma((ITERS + 1, blocks)),
-            dma((nz,)), dma((nz,)), dma((tm,)), dma((tm,)),
+            dma((nz,)), dma((nz,)), dma((1,)), dma((1,)),
         ],
         compiler_params=pltpu.CompilerParams(collective_id=0, has_side_effects=True),
         name="parareal",

time: 78.2 us -> 73.1 us (0.935)
  Pallas kernels: 75.3 us -> 70.9 us
  local copies, waits for them, and re-layouts: 2.17 us -> 1.25 us
    pallas_call x1, Pallas kernels: 75.3 us -> 70.9 us  [body(): pl.pallas_call(functools.partial(kernel, tm, env), out_shape=(vm((STATE,...]
    unnamed x4 -> x2, local copies, waits for them, and re-layouts: 2.17 us -> 1.25 us
where the time goes in v4:
time: 73.1 us; the launch traced here: 72.8 us
  Pallas kernels  70.9 us (97%)
  local copies, waits for them, and re-layouts  1.25 us (2%)
    pallas_call x1, Pallas kernels, body(): pl.pallas_call(functools.partial(kernel, tm, env), out_shape=(vm((STATE,...  70.9 us

profile of v4, /device:TPU:1, one launch (start us, length us, event | category | flops | bytes accessed | tf_op | source)
XLA Modules:
  0.0 72.8 jit_solution(12001680855452383275)
XLA Ops:
  0.6 70.9 %parareal.1 = (f32[70,2,256]{2,1,0:T(2,128)S(1)}, f32[3,256]{1,0:T(4,128)S(1)}) custom-call(f32[70,256]{1,0:T(8,128)} %init_hbm.1, f32[35,4,256]{2,1,0:T(4,128)} %bitcast.9, s32[4,256]{1,0:T(4,128)} %contact_hbm.1, f32[35,2,35]{2,1,0:T(2,128)} %bitcast.10, f32[1,35]{1,0:T(1,128)} %bitcast.11, f32[1,35]{1,0:T(1,128)} %bitcast.12, f32[1,35]{1,0:T(1,128)} %bitcast.13, ...), custom_call_target="tpu_custom_call" | custom-call | tf_op jit(solution)/shard_map/parareal/pallas_call | solution.py:753
  71.5 0.7 copy.13
  72.2 0.6 copy.14

commit v5 on v4

--- a/solution.py
+++ b/solution.py
@@ -106,7 +106,7 @@
     out, corr_out,
     init, torque, contact, minv, stiff, damp, gravity, cstiff, cdamp,
     tx, rx, mtx, mrx, rowtx, rows, raw, inits,
-    tstage, gains, tq, spring, fric, grav, cspring, cfric, wgt, stage, wtmp, ybuf, ubuf, ly, lu,
+    tstage, hstage, gains, tq, spring, fric, grav, cspring, cfric, wgt, stage, wtmp, ybuf, ubuf, ly, lu,
     cmap, qmap, bmap, ctmp, xs, ends_buf,
     btx, brx, stx, srx, otx, orx, ctx, crx,
     lsem, tsend, trecv, msend, mrecv, rsend, rrecv, bsend, brecv, ssend, srecv, osend, orecv, csend, crecv,
@@ -207,7 +207,7 @@
         return pltpu.make_async_remote_copy(
             src_ref=tx.at[lax.rem(z + k, nz)],
             dst_ref=rx.at[my_source],
-            send_sem=tsend.at[k],
+            send_sem=tsend.at[0],
             recv_sem=trecv.at[my_source],
             device_id={"tm": dest_index(k), "env": me_e},
             device_id_type=MESH,
@@ -227,7 +227,7 @@
         return pltpu.make_async_remote_copy(
             src_ref=mtx,
             dst_ref=mrx.at[my_source],
-            send_sem=msend.at[k],
+            send_sem=msend.at[0],
             recv_sem=mrecv.at[my_source],
             device_id={"tm": dest_index(k), "env": me_e},
             device_id_type=MESH,
@@ -290,7 +290,7 @@
     scale = jnp.where(lane_of < DOF, TWO_PI, to_u)
     shrink = jnp.where(lane_of < DOF, 1.0 / TWO_PI, 1.0 / to_u)
 
-    for ref in (tstage, gains, tq, spring, fric, grav, cspring, cfric, ybuf, ubuf, ly, lu, ctmp, stage, wgt, cmap, qmap, bmap):
+    for ref in (tstage, hstage, gains, tq, spring, fric, grav, cspring, cfric, ybuf, ubuf, ly, lu, ctmp, stage, wgt, cmap, qmap, bmap):
         clear(ref)
     for h in range(tiles):
         inits[h * LANES : (h + 1) * LANES, :] = (
@@ -383,9 +383,14 @@
         for m in range(0, slices, 2 * step):
             for i in range(step):
                 found.append((level * (slices // 2) + len(found), m + step - 1, m + step + i))
-        if level == levels - 1:
-            found = found[-1:] + found[:-1]
         return found
+
+    def steps(spine):
+        return [
+            [entry for entry in right_half(level) if ((entry[2] + 1) % (2 << level) == 0) == spine]
+            for level in range(levels)
+        ]
+
 
     for level in range(levels):
         for place, left, n in right_half(level):
@@ -397,12 +402,15 @@
         put(qmap, n, stacks[n])
 
     def sweep(ends, k):
-        for level in range(levels):
-            for place, left, n in right_half(level):
-                ends[n] = ends[n] + through(ends[left], cmap[place])
-                if n == slices - 1 and level == levels - 1:
-                    stx[k] = ends[n]
-                    send_blocks(functools.partial(sweep_copy, k))
+        def advance(spine):
+            for entries in steps(spine):
+                for place, left, n in entries:
+                    ends[n] = ends[n] + through(ends[left], cmap[place])
+
+        advance(True)
+        stx[k] = ends[slices - 1]
+        send_blocks(functools.partial(sweep_copy, k))
+        advance(False)
         for n in range(slices):
             ends_buf[n] = ends[n]
 
@@ -410,19 +418,9 @@
         return pltpu.make_async_remote_copy(
             src_ref=btx,
             dst_ref=brx.at[block_t],
-            send_sem=bsend.at[d],
-            recv_sem=brecv.at[d],
+            send_sem=bsend.at[0],
+            recv_sem=brecv.at[0],
             device_id={"tm": block_index(block_t + d), "env": me_e},
-            device_id_type=MESH,
-        )
-
-    def first_arrival(d):
-        return pltpu.make_async_remote_copy(
-            src_ref=btx,
-            dst_ref=brx.at[block_t - d],
-            send_sem=bsend.at[d],
-            recv_sem=brecv.at[d],
-            device_id={"tm": block_index(block_t - d), "env": me_e},
             device_id_type=MESH,
         )
 
@@ -430,48 +428,47 @@
         return pltpu.make_async_remote_copy(
             src_ref=stx.at[k],
             dst_ref=srx.at[k, block_t],
-            send_sem=ssend.at[k, d],
-            recv_sem=srecv.at[k, d],
+            send_sem=ssend.at[k],
+            recv_sem=srecv.at[k],
             device_id={"tm": block_index(block_t + d), "env": me_e},
             device_id_type=MESH,
         )
 
-    def sweep_arrival(k, d):
-        return pltpu.make_async_remote_copy(
-            src_ref=stx.at[k],
-            dst_ref=srx.at[k, block_t - d],
-            send_sem=ssend.at[k, d],
-            recv_sem=srecv.at[k, d],
-            device_id={"tm": block_index(block_t - d), "env": me_e},
-            device_id_type=MESH,
-        )
+    def whole_copy(ref, send, recv):
+        return pltpu.make_async_remote_copy(
+            src_ref=ref, dst_ref=ref, send_sem=send, recv_sem=recv,
+            device_id={"tm": block_index(lax.rem(block_t + 1, blocks)), "env": me_e},
+            device_id_type=MESH,
+        )
+
+    def first_whole(count):
+        return whole_copy(brx.at[pl.ds(0, count)], bsend.at[0], brecv.at[0])
+
+    def sweep_whole(k, count):
+        return whole_copy(srx.at[k, pl.ds(0, count)], ssend.at[k], srecv.at[k])
 
     def send_blocks(copy):
-        @pl.loop(1, blocks)
-        def _(d):
+        for d in range(1, blocks):
             @pl.when(block_t + d < blocks)
-            def _():
+            def _(d=d):
                 copy(d).start()
 
-    def await_blocks(arrival):
-        @pl.loop(1, blocks)
-        def _(d):
-            @pl.when(block_t - d >= 0)
-            def _():
-                arrival(d).wait_recv()
-
-    def drain_blocks(copy):
-        @pl.loop(1, blocks)
-        def _(d):
-            @pl.when(block_t + d < blocks)
-            def _():
-                copy(d).wait_send()
+    def await_blocks(whole, skip=0):
+        for count in range(1, blocks - skip):
+            @pl.when(block_t - skip == count)
+            def _(count=count):
+                whole(count).wait_recv()
+
+    def drain_blocks(whole):
+        for count in range(1, blocks):
+            @pl.when(blocks - 1 - block_t == count)
+            def _(count=count):
+                whole(count).wait_send()
 
     @pl.when(block_t > 0)
     def _():
         send_blocks(first_copy)
 
-    mark = plan.per * DOF
     for part in range(0, nz, plan.per):
         for pos, i in enumerate(range(part, min(part + plan.per, nz))):
             @pl.when(other_source(i))
@@ -479,18 +476,18 @@
                 in_arrival(i).wait_recv()
 
             tstage[part // plan.per, pos * DOF : (pos + 1) * DOF, :] = rx[i, 0:DOF, :]
-            tstage[part // plan.per, mark + pos : mark + pos + 1, :] = rx[i, DOF : DOF + 1, :]
+            hstage[part // plan.per, pos * DOF : (pos + 1) * DOF, :] = jnp.broadcast_to(
+                rx[i, DOF : DOF + 1, :], (DOF, LANES)
+            )
         turned = tstage[part // plan.per].T
+        touched = hstage[part // plan.per].T
         for a in range(HS):
             base = (part // plan.per * HS + a) * LANES
             cut = pl.ds(base, LANES)
             for j in range(HS):
                 k = a * HS + j
-                piece = turned[k * epd : (k + 1) * epd, :]
-                hit = piece[:, mark : mark + 1]
-                for pos in range(1, plan.per):
-                    hit = jnp.where(lane_of >= pos * DOF, piece[:, mark + pos : mark + pos + 1], hit)
-                tq[j, :, cut] = jnp.where(lane_of < mark, piece, 0.0)
+                hit = touched[k * epd : (k + 1) * epd, :]
+                tq[j, :, cut] = turned[k * epd : (k + 1) * epd, :]
                 spring[j, :, cut] = gains[0, :, cut] + hit * gains[1, :, cut]
                 fric[j, :, cut] = gains[2, :, cut] + hit * gains[3, :, cut]
 
@@ -511,12 +508,7 @@
 
     ends = [packed_state(n) for n in range(slices)]
     sweep(ends, 0)
-    @pl.loop(1, blocks)
-    def _(d):
-        @pl.when(block_t - d > 0)
-        def _():
-            first_arrival(d).wait_recv()
-
+    await_blocks(first_whole, 1)
     eye = jnp.where(
         lax.broadcasted_iota(jnp.int32, (DEPTH, LANES), 0) == lane_of, 1.0, 0.0
     )
@@ -552,7 +544,7 @@
             total = total + through(jnp.where(t < block_t, srx[k, t], 0.0), bmap[weights[t + 1, top]])
         return total
 
-    await_blocks(functools.partial(sweep_arrival, 0))
+    await_blocks(functools.partial(sweep_whole, 0))
     entry = enter(0)
     xs[0] = jnp.where(block_t == 0, start_state, entry)
     for n in range(slices):
@@ -573,16 +565,15 @@
                     t = y - jnp.round(y)
                     s = t * t
                     s2 = s * s
-                    poly = (SIN[0] + SIN[1] * s) + s2 * ((SIN[2] + SIN[3] * s) + s2 * (SIN[4] + SIN[5] * s))
+                    poly = ((SIN[0] + SIN[1] * s) + s2 * (SIN[2] + SIN[3] * s)) + (s2 * s2) * (SIN[4] + SIN[5] * s)
                     force = (
                         tq[j, :, cut]
                         - spring[j, :, cut] * y
                         - fric[j, :, cut] * u
                         - (grav[:, cut] * t) * poly
                     )
-                    u = u + product(force, g)
-                    y = y + u
-                    result.append((y, u))
+                    change = product(force, g)
+                    result.append(((y + u) + change, u + change))
                 return tuple(result)
 
             first_state = tuple(
@@ -596,7 +587,7 @@
 
         ends = [packed_state(n) - xs[n + 1] for n in range(slices)]
         sweep(ends, k + 1)
-        await_blocks(functools.partial(sweep_arrival, k + 1))
+        await_blocks(functools.partial(sweep_whole, k + 1))
         entry = enter(k + 1)
         xs[0] = xs[0] + entry
         worst = jnp.zeros((epd, 1), F32)
@@ -626,7 +617,7 @@
         return pltpu.make_async_remote_copy(
             src_ref=otx.at[i],
             dst_ref=orx.at[z],
-            send_sem=osend.at[i],
+            send_sem=osend.at[0],
             recv_sem=orecv.at[z],
             device_id={"tm": source_index(i), "env": me_e},
             device_id_type=MESH,
@@ -711,26 +702,27 @@
                 tile = v if tile is None else jnp.where(lane_group == q, v, tile)
             corr_out[k : k + 1, h * LANES : (h + 1) * LANES] = tile
 
-    @pl.loop(0, nz)
-    def _(k):
-        @pl.when(other(k))
-        def _():
-            in_copy(k).wait_send()
-            mat_copy(k).wait_send()
-
-        @pl.when(other_source(k))
-        def _():
-            out_copy(k).wait_send()
+    def drain(ref, sem, count):
+        whole_copy(ref.at[pl.ds(0, count)], sem.at[0], sem.at[0]).wait_send()
+
+    for ref, sem in ((mrx, msend), (tx, tsend), (otx, osend)):
+        @pl.when(own_here)
+        def _(ref=ref, sem=sem):
+            drain(ref, sem, nz - 1)
+
+        @pl.when(jnp.logical_not(own_here))
+        def _(ref=ref, sem=sem):
+            drain(ref, sem, nz)
 
     if ny > 1:
         rows_all().wait_send()
 
     @pl.when(block_t > 0)
     def _():
-        drain_blocks(first_copy)
+        drain_blocks(first_whole)
 
     for k in range(ITERS + 1):
-        drain_blocks(functools.partial(sweep_copy, k))
+        drain_blocks(functools.partial(sweep_whole, k))
 
 
 def body(tm, env, init_state, torque, contact, mass_inverse, stiffness, damping, gravity,
@@ -765,7 +757,7 @@
             vm((ROWS_MAT, LANES), F32), vm((nz, ROWS_MAT, LANES), F32),
             vm((1, LANES), F32), vm((env, nz, 1, LANES), F32),
             vm((2 * HS, 40, env_local), F32), vm((env_local, LANES), F32),
-            vm((-(-nz // plan.per), LANES, LANES), F32), vm((5, 1, lanes), F32),
+            *[vm((-(-nz // plan.per), LANES, LANES), F32)] * 2, vm((5, 1, lanes), F32),
             both, both, both, vm((1, lanes), F32), thin, thin,
             vm((groups, WIDE, WIDE), BF16), vm((groups, LANES, LANES), F32), vm((LANES, LANES), F32),
             vm((epd, lanes), F32), vm((epd, lanes), F32),
@@ -778,9 +770,9 @@
             vm((ITERS + 1, epd, LANES), F32), vm((ITERS + 1, blocks, epd, LANES), F32),
             vm((nz, ROWS_OUT, LANES), F32), vm((nz, ROWS_OUT, LANES), F32),
             vm((1, LANES), F32), vm((tm, 1, LANES), F32),
-            dma((9,)), dma((nz,)), dma((nz,)), dma((nz,)), dma((nz,)), dma((1,)), dma((1,)),
-            dma((blocks,)), dma((blocks,)), dma((ITERS + 1, blocks)), dma((ITERS + 1, blocks)),
-            dma((nz,)), dma((nz,)), dma((1,)), dma((1,)),
+            dma((9,)), dma((1,)), dma((nz,)), dma((1,)), dma((nz,)), dma((1,)), dma((1,)),
+            dma((1,)), dma((1,)), dma((ITERS + 1,)), dma((ITERS + 1,)),
+            dma((1,)), dma((nz,)), dma((1,)), dma((1,)),
         ],
         compiler_params=pltpu.CompilerParams(collective_id=0, has_side_effects=True),
         name="parareal",

time: 73.1 us -> 71.3 us (0.975)
  Pallas kernels: 70.9 us -> 69.1 us
    pallas_call x1, Pallas kernels: 70.9 us -> 69.1 us  [body(): pl.pallas_call(functools.partial(kernel, tm, env), out_shape=(vm((STATE,...]
where the time goes in v5:
time: 71.3 us; the launch traced here: 71 us
  Pallas kernels  69.1 us (97%)
  local copies, waits for them, and re-layouts  1.25 us (2%)
    pallas_call x1, Pallas kernels, body(): pl.pallas_call(functools.partial(kernel, tm, env), out_shape=(vm((STATE,...  69.1 us

profile of v5, /device:TPU:1, one launch (start us, length us, event | category | flops | bytes accessed | tf_op | source)
XLA Modules:
  0.0 71.0 jit_solution(3747090061389826982)
XLA Ops:
  0.6 69.1 %parareal.1 = (f32[70,2,256]{2,1,0:T(2,128)S(1)}, f32[3,256]{1,0:T(4,128)S(1)}) custom-call(f32[70,256]{1,0:T(8,128)} %init_hbm.1, f32[35,4,256]{2,1,0:T(4,128)} %bitcast.9, s32[4,256]{1,0:T(4,128)} %contact_hbm.1, f32[35,2,35]{2,1,0:T(2,128)} %bitcast.10, f32[1,35]{1,0:T(1,128)} %bitcast.11, f32[1,35]{1,0:T(1,128)} %bitcast.12, f32[1,35]{1,0:T(1,128)} %bitcast.13, ...), custom_call_target="tpu_custom_call" | custom-call | tf_op jit(solution)/shard_map/parareal/pallas_call | solution.py:745
  69.7 0.7 copy.13
  70.4 0.6 copy.14

commit v6 on v5

--- a/solution.py
+++ b/solution.py
@@ -107,7 +107,7 @@
     init, torque, contact, minv, stiff, damp, gravity, cstiff, cdamp,
     tx, rx, mtx, mrx, rowtx, rows, raw, inits,
     tstage, hstage, gains, tq, spring, fric, grav, cspring, cfric, wgt, stage, wtmp, ybuf, ubuf, ly, lu,
-    cmap, qmap, bmap, ctmp, xs, ends_buf,
+    cmap, qmap, bmap, ctmp, xs, ends_buf, changes,
     btx, brx, stx, srx, otx, orx, ctx, crx,
     lsem, tsend, trecv, msend, mrecv, rsend, rrecv, bsend, brecv, ssend, srecv, osend, orecv, csend, crecv,
 ):
@@ -290,7 +290,7 @@
     scale = jnp.where(lane_of < DOF, TWO_PI, to_u)
     shrink = jnp.where(lane_of < DOF, 1.0 / TWO_PI, 1.0 / to_u)
 
-    for ref in (tstage, hstage, gains, tq, spring, fric, grav, cspring, cfric, ybuf, ubuf, ly, lu, ctmp, stage, wgt, cmap, qmap, bmap):
+    for ref in (changes, tstage, hstage, gains, tq, spring, fric, grav, cspring, cfric, ybuf, ubuf, ly, lu, ctmp, stage, wgt, cmap, qmap, bmap):
         clear(ref)
     for h in range(tiles):
         inits[h * LANES : (h + 1) * LANES, :] = (
@@ -549,6 +549,13 @@
     xs[0] = jnp.where(block_t == 0, start_state, entry)
     for n in range(slices):
         xs[n + 1] = ends_buf[n] + through(entry, qmap[n])
+
+    def largest(k, corrections):
+        worst = jnp.zeros((epd, 1), F32)
+        for n in range(slices):
+            real = changes[n] * scale
+            worst = jnp.maximum(worst, jnp.sum(real * real, axis=1, keepdims=True))
+        return jnp.where(lane_of == k, jnp.sqrt(worst), corrections)
 
     def iteration(k, corrections):
         for n in range(slices):
@@ -587,24 +594,39 @@
 
         ends = [packed_state(n) - xs[n + 1] for n in range(slices)]
         sweep(ends, k + 1)
+        corrections = largest(k - 1, corrections)
         await_blocks(functools.partial(sweep_whole, k + 1))
         entry = enter(k + 1)
         xs[0] = xs[0] + entry
-        worst = jnp.zeros((epd, 1), F32)
         for n in range(slices):
             change = ends_buf[n] + through(entry, qmap[n])
-            real = change * scale
-            worst = jnp.maximum(worst, jnp.sum(real * real, axis=1, keepdims=True))
+            changes[n] = change
             xs[n + 1] = xs[n + 1] + change
-        return jnp.where(lane_of == k, jnp.sqrt(worst), corrections)
+        return corrections
 
     corrections = lax.fori_loop(0, ITERS, iteration, jnp.zeros((epd, LANES), F32))
+    corrections = largest(ITERS - 1, corrections)
 
     turned = pad_rows(corrections, LANES).T
     row = turned[0:1]
     for k in range(1, ITERS):
         row = jnp.where(lane_group == k, pltpu.roll(turned[k : k + 1], k * epd, 1), row)
     ctx[...] = row
+
+    def corr_copy(k):
+        return pltpu.make_async_remote_copy(
+            src_ref=ctx,
+            dst_ref=crx.at[k],
+            send_sem=csend.at[0],
+            recv_sem=crecv.at[0],
+            device_id={"tm": lax.rem(me_t + k, tm), "env": me_e},
+            device_id_type=MESH,
+        )
+
+    @pl.loop(1, tm, unroll=True)
+    def _(k):
+        corr_copy(k).start()
+
     for i in range(nz):
         parts = []
         for a in range(HS):
@@ -632,20 +654,6 @@
             device_id={"tm": dest_index(k), "env": me_e},
             device_id_type=MESH,
         )
-
-    def corr_copy(k):
-        return pltpu.make_async_remote_copy(
-            src_ref=ctx,
-            dst_ref=crx.at[k],
-            send_sem=csend.at[0],
-            recv_sem=crecv.at[0],
-            device_id={"tm": lax.rem(me_t + k, tm), "env": me_e},
-            device_id_type=MESH,
-        )
-
-    @pl.loop(1, tm, unroll=True)
-    def _(k):
-        corr_copy(k).start()
 
     @pl.loop(0, nz)
     def _(i):
@@ -765,7 +773,7 @@
             vm((levels * slices // 2, WIDE, WIDE), BF16),
             vm((slices, WIDE, WIDE), BF16), vm((2 * blocks, WIDE, WIDE), BF16),
             vm((DEPTH, LANES), F32),
-            vm((slices + 1, epd, LANES), F32), vm((slices, epd, LANES), F32),
+            vm((slices + 1, epd, LANES), F32), vm((slices, epd, LANES), F32), vm((slices, epd, LANES), F32),
             vm((ROWS_MAP, LANES), F32), vm((blocks, ROWS_MAP, LANES), F32),
             vm((ITERS + 1, epd, LANES), F32), vm((ITERS + 1, blocks, epd, LANES), F32),
             vm((nz, ROWS_OUT, LANES), F32), vm((nz, ROWS_OUT, LANES), F32),

time: 71.3 us -> 70.9 us (level)
  no operation moved by 1% of the time
where the time goes in v6:
time: 70.9 us; the launch traced here: 70.7 us
  Pallas kernels  68.8 us (97%)
  local copies, waits for them, and re-layouts  1.25 us (2%)
    pallas_call x1, Pallas kernels, body(): pl.pallas_call(functools.partial(kernel, tm, env), out_shape=(vm((STATE,...  68.8 us

profile of v6, /device:TPU:1, one launch (start us, length us, event | category | flops | bytes accessed | tf_op | source)
XLA Modules:
  0.0 70.7 jit_solution(3656231369646731581)
XLA Ops:
  0.6 68.8 %parareal.1 = (f32[70,2,256]{2,1,0:T(2,128)S(1)}, f32[3,256]{1,0:T(4,128)S(1)}) custom-call(f32[70,256]{1,0:T(8,128)} %init_hbm.1, f32[35,4,256]{2,1,0:T(4,128)} %bitcast.9, s32[4,256]{1,0:T(4,128)} %contact_hbm.1, f32[35,2,35]{2,1,0:T(2,128)} %bitcast.10, f32[1,35]{1,0:T(1,128)} %bitcast.11, f32[1,35]{1,0:T(1,128)} %bitcast.12, f32[1,35]{1,0:T(1,128)} %bitcast.13, ...), custom_call_target="tpu_custom_call" | custom-call | tf_op jit(solution)/shard_map/parareal/pallas_call | solution.py:753
  69.5 0.7 copy.13
  70.1 0.6 copy.14

commit v7 on v6

--- a/solution.py
+++ b/solution.py
@@ -146,24 +146,23 @@
     def block_index(t):
         return t // CORES * line + z * CORES + lax.rem(t, CORES)
 
-    @pl.loop(1, tm, unroll=True)
-    def _(k):
-        pl.semaphore_signal(
-            barrier, inc=1, device_id={"tm": lax.rem(me_t + k, tm), "env": me_e}, device_id_type=MESH
-        )
-
-    for copy in local:
-        copy.start()
-
-    @pl.loop(1, ny)
-    def _(r):
+    for r in range(1, ny):
         @pl.loop(0, nz, unroll=True)
-        def _(i):
+        def _(i, r=r):
             pl.semaphore_signal(
                 barrier, inc=1,
                 device_id={"tm": source_index(i), "env": lax.rem(me_e + r, ny)},
                 device_id_type=MESH,
             )
+
+    @pl.loop(1, tm, unroll=True)
+    def _(k):
+        pl.semaphore_signal(
+            barrier, inc=1, device_id={"tm": lax.rem(me_t + k, tm), "env": me_e}, device_id_type=MESH
+        )
+
+    for copy in local:
+        copy.start()
 
     for copy in local:
         copy.wait()

time: 70.9 us -> 70.4 us (level)
  no operation moved by 1% of the time
where the time goes in v7:
time: 70.4 us; the launch traced here: 70.3 us
  Pallas kernels  68.4 us (97%)
  local copies, waits for them, and re-layouts  1.25 us (2%)
    pallas_call x1, Pallas kernels, body(): pl.pallas_call(functools.partial(kernel, tm, env), out_shape=(vm((STATE,...  68.4 us

profile of v7, /device:TPU:1, one launch (start us, length us, event | category | flops | bytes accessed | tf_op | source)
XLA Modules:
  0.0 70.3 jit_solution(15628240931919676648)
XLA Ops:
  0.6 68.4 %parareal.1 = (f32[70,2,256]{2,1,0:T(2,128)S(1)}, f32[3,256]{1,0:T(4,128)S(1)}) custom-call(f32[70,256]{1,0:T(8,128)} %init_hbm.1, f32[35,4,256]{2,1,0:T(4,128)} %bitcast.9, s32[4,256]{1,0:T(4,128)} %contact_hbm.1, f32[35,2,35]{2,1,0:T(2,128)} %bitcast.10, f32[1,35]{1,0:T(1,128)} %bitcast.11, f32[1,35]{1,0:T(1,128)} %bitcast.12, f32[1,35]{1,0:T(1,128)} %bitcast.13, ...), custom_call_target="tpu_custom_call" | custom-call | tf_op jit(solution)/shard_map/parareal/pallas_call | solution.py:752
  69.0 0.7 copy.13
  69.7 0.6 copy.14
